TPU v7x, 128 devices: a whole 4x4x4 slice. The times are simulated.
128 devices in a mesh: dp: 8 (over y_lo, z), head: 16 (over x, y_hi, core).
Axes of the slice: x: 4, y: 4 (y_hi: 2, y_lo: 2; y = y_hi * 2 + y_lo), z: 4, core: 2. Of those that a mesh axis runs over, the one named last changes fastest.
Arguments:
- projected: bfloat16 [49152, 24576], P(('dp', 'head')), may hold values from -64 to 64, as said below
- weight_exp: int32 [49152], P(('dp', 'head')), may hold values from 0 to 3
- damp_exp: int32 [128], replicated, may hold values from 0 to 2
Outputs:
- whitening: float32 [128, 192, 192], P('head')
Inputs may be any that keep to these rules, and one draw needn't show every extreme that they name: `projected`: real values.
All inputs are finite; a program needn't handle non-finite values.
Results may differ from a plain program's by a relative error of at most 0.0003.
Values may be sent and summed in bfloat16 or wider, within the bound.
No kernel may reach another device: no remote copies, remote signals or barrier semaphores. Data moves between devices by JAX's collectives and lax.ppermute only.
A program may use at most 192 MiB of HBM per device.

v0:
```python
import jax
import jax.numpy as jnp
from jax import lax
from jax.experimental import pallas as pl
from jax.experimental.pallas import tpu as pltpu
from jax.sharding import PartitionSpec as P

HD = 192
HALF = 64
LANES = 128
ROWS = 152
OUT_ROWS = 192
TOKENS = 49152
DEVICES = ("dp", "head")


def place(device):
    dp, head = divmod(device, 16)
    y_lo, z = divmod(dp, 4)
    x, y_hi, core = head // 4, head // 2 % 2, head % 2
    return x, 2 * y_hi + y_lo, z, core


def near(v):
    return v >> 1


def far(v):
    return (v >> 1) ^ (v & 1)


def cubes(stage):
    groups = {}
    for device in range(128):
        x, y, z, core = place(device)
        inner = (near(x), near(y), near(z))
        outer = (far(x), far(y), far(z))
        key, member = (inner, outer) if (core == 0) == (stage == 0) else (outer, inner)
        first = member[0] if stage == 0 else member[0] ^ key[0]
        groups.setdefault((core, key), [0] * 8)[first * 4 + member[1] * 2 + member[2]] = device
    return [groups[k] for k in sorted(groups)]


def partner_pairs():
    return [(d, d ^ 1) for d in range(128)]


def peers(flip):
    pairs = []
    for group in cubes(0):
        pairs += [(group[i], group[i ^ flip]) for i in range(8)]
    return sorted(pairs)


def owner_groups():
    return [[dp * 16 + head for dp in range(8)] for head in range(16)]


def chunk_block(half, i):
    return (i >> 1) * 4 + half * 2 + (i & 1)


def spot(block, inner, core):
    x, y_hi = block >> 1, block & 1
    y_lo, z = inner >> 2, inner & 3
    y = 2 * y_hi + y_lo
    a, a_rest = near(x) * 4 + near(y) * 2 + near(z), near(y) * 2 + near(z)
    b, b_rest = far(x) * 4 + far(y) * 2 + far(z), far(y) * 2 + far(z)
    return jnp.where(core == 0, b * 4 + a_rest, a * 4 + b_rest)


def on_chip(v):
    return pltpu.with_memory_space_constraint(v, pltpu.VMEM)


def off_chip(v):
    return pltpu.with_memory_space_constraint(v, pltpu.HBM)


WHOLE = pl.BlockSpec(memory_space=pltpu.VMEM)


def params(mebibytes, **kwargs):
    return pltpu.CompilerParams(vmem_limit_bytes=mebibytes << 20, **kwargs)


def rolled(v, by):
    return pltpu.roll(v, by, 1)


def block_grams(x_ref, w_ref, put):
    w = w_ref[...]
    w3 = jnp.concatenate([w, w, w], axis=1)
    row = lax.broadcasted_iota(jnp.int32, (HALF, LANES), 0)
    lane = lax.broadcasted_iota(jnp.int32, (HALF, LANES), 1)
    row32, lane32 = row[:32], lane[:32]
    row16, lane16 = row[:16], lane[:16]
    row8 = row[:8]
    contract = (((0,), (0,)), ((), ()))

    def finish(index, low, mid, first, last, at):
        put(index, 0, low)
        put(index, 64, jnp.where(lane - HALF > row, first, mid))

        def moved(v, to):
            return v if to == at else rolled(v, (to - at) % LANES)

        near_half = jnp.where(lane16 - 32 > row16, moved(last[:16], 32), moved(last[32:48], 0))
        far_half = jnp.where(lane16 - 96 > row16 + 16, moved(last[16:32], 96), moved(last[48:64], HALF))
        put(index, 128, jnp.where(lane16 < HALF, near_half, far_half))
        diag = jnp.sum(jnp.where(lane - HALF == row, first, 0.0), axis=0, keepdims=True)
        small = jnp.sum(jnp.where(lane32 - at == row32, last[:32], 0.0), axis=0, keepdims=True)
        diag = jnp.broadcast_to(diag, (8, LANES)) + moved(jnp.broadcast_to(small, (8, LANES)), 0)
        put(index, 144, jnp.where(row8 == 0, diag, 0.0))

    for pair in range(4):
        x = x_ref[:, 384 * pair : 384 * (pair + 1)]
        xw = x * w3
        g = lax.dot_general(x[:, :256], xw[:, :256], contract, preferred_element_type=jnp.float32)
        f = lax.dot_general(x[:, 256:], xw[:, 128:], contract, preferred_element_type=jnp.float32)
        finish(2 * pair, g[128:192, :128], g[64:128, :128], rolled(g[:64, :128], HALF), g[128:192, 128:], 0)
        swapped = jnp.where(lane < HALF, f[64:, 128:], f[64:, :128])
        middle = jnp.where(lane < HALF, f[:64, 128:], f[:64, :128])
        finish(2 * pair + 1, rolled(swapped, HALF), rolled(middle, HALF), g[192:, 128:], f[64:, 128:], HALF)


def spread_weights(exp_ref, w_ref):
    for i in range(exp_ref.shape[0] // LANES):
        power = (1 << exp_ref[LANES * i : LANES * (i + 1)].reshape(1, LANES)).astype(jnp.float32)
        w_ref[LANES * i : LANES * (i + 1)] = jnp.broadcast_to(power, (LANES, LANES)).T.astype(jnp.bfloat16)


def their_grams_kernel(core_ref, x_ref, exp_ref, o_ref, w_ref):
    @pl.when(pl.program_id(0) == 0)
    def _():
        spread_weights(exp_ref, w_ref)

    i = pl.program_id(0)

    def put(index, start, rows):
        o_ref[8 * i + index, start : start + rows.shape[0]] = rows

    block_grams(x_ref, w_ref, put)


def their_grams(projected, weight_exp, core, half):
    tokens = projected.shape[0]
    return pl.pallas_call(
        their_grams_kernel,
        grid_spec=pltpu.PrefetchScalarGridSpec(
            num_scalar_prefetch=1,
            grid=(4,),
            in_specs=[
                pl.BlockSpec((tokens, 8 * HD), lambda i, core: (0, 2 * chunk_block(half, i) + 1 - core[0])),
                pl.BlockSpec((tokens,), lambda i, core: (0,)),
            ],
            out_specs=WHOLE,
            scratch_shapes=[pltpu.VMEM((tokens, LANES), jnp.bfloat16)],
        ),
        out_shape=pltpu.VMEM((32, ROWS, LANES), jnp.float32),
        compiler_params=params(12, dimension_semantics=("arbitrary",)),
        cost_estimate=pl.CostEstimate(flops=tokens * 64 * HD * HD, bytes_accessed=7_500_000, transcendentals=0),
        name="their_grams",
    )(core, off_chip(projected), off_chip(weight_exp))


def my_even_kernel(core_ref, spot_ref, x_ref, exp_ref, received_ref, o_ref, w_ref):
    fill_slots(0, core_ref, x_ref, exp_ref, received_ref, o_ref, w_ref)


def fill_slots(half, core_ref, x_ref, exp_ref, received_ref, o_ref, w_ref):
    i = pl.program_id(0)

    @pl.when(i == 0)
    def _():
        spread_weights(exp_ref, w_ref)

    block = chunk_block(half, i)
    slots = [spot(block, inner, core_ref[0]) for inner in range(8)]

    def put(index, start, rows):
        size = rows.shape[0]
        o_ref[slots[index], start : start + size] = rows + received_ref[8 * i + index, start : start + size]

    block_grams(x_ref, w_ref, put)


def my_odd_kernel(core_ref, spot_ref, x_ref, exp_ref, received_ref, *refs):
    outs, (w_ref, all_ref) = refs[:8], refs[8:]
    fill_slots(1, core_ref, x_ref, exp_ref, received_ref, all_ref, w_ref)

    @pl.when(pl.program_id(0) == pl.num_programs(0) - 1)
    def _():
        for flip in range(8):
            slot = spot_ref[0] ^ flip
            for i in range(4):
                outs[flip][i] = all_ref[slot * 4 + i]


def my_grams(projected, weight_exp, received, core, own_spot, half):
    tokens = projected.shape[0]

    scratch = [pltpu.VMEM((tokens, LANES), jnp.bfloat16)]
    if half:
        kernel, outs = my_odd_kernel, [WHOLE] * 8
        shapes = [pltpu.VMEM((4, ROWS, LANES), jnp.float32)] * 8
        scratch.append(pltpu.VMEM((32, ROWS, LANES), jnp.float32))
    else:
        kernel, outs = my_even_kernel, WHOLE
        shapes = pltpu.HBM((32, ROWS, LANES), jnp.float32)
    return pl.pallas_call(
        kernel,
        grid_spec=pltpu.PrefetchScalarGridSpec(
            num_scalar_prefetch=2,
            grid=(4,),
            in_specs=[
                pl.BlockSpec((tokens, 8 * HD), lambda i, core, spot: (0, 2 * chunk_block(half, i) + core[0])),
                pl.BlockSpec((tokens,), lambda i, core, spot: (0,)),
                WHOLE,
            ],
            out_specs=outs,
            scratch_shapes=scratch,
        ),
        out_shape=shapes,
        compiler_params=params(16, dimension_semantics=("arbitrary",)),
        cost_estimate=pl.CostEstimate(flops=tokens * 64 * HD * HD, bytes_accessed=10_000_000, transcendentals=0),
        name="my_grams",
    )(core, own_spot, off_chip(projected), off_chip(weight_exp), on_chip(received))


def even_kernel(even_ref, o_ref):
    total = even_ref[0, 0]
    for k in range(1, 8):
        total = total + even_ref[k, 0]
    o_ref[pl.program_id(0)] = total


def add_even(even):
    return pl.pallas_call(
        even_kernel,
        grid=(4,),
        in_specs=[pl.BlockSpec((8, 1, ROWS, LANES), lambda i: (0, i, 0, 0))],
        out_specs=WHOLE,
        out_shape=pltpu.VMEM((4, ROWS, LANES), jnp.float32),
        compiler_params=params(8, dimension_semantics=("arbitrary",)),
        cost_estimate=pl.CostEstimate(flops=6_000_000, bytes_accessed=3_000_000, transcendentals=0),
        name="add_even",
    )(off_chip(even))


def odd_kernel(even_ref, *refs):
    odd_refs, o_ref = refs[:8], refs[8]

    def one(i, carry):
        o_ref[i] = even_ref[i]
        total = odd_refs[0][i]
        for k in range(1, 8):
            total = total + odd_refs[k][i]
        o_ref[4 + i] = total
        return carry

    lax.fori_loop(0, 4, one, 0)


def add_odd(even_sum, odd):
    return pl.pallas_call(
        odd_kernel,
        in_specs=[WHOLE] * 9,
        out_specs=WHOLE,
        out_shape=pltpu.VMEM((8, ROWS, LANES), jnp.float32),
        compiler_params=params(8),
        name="add_odd",
    )(on_chip(even_sum), *[on_chip(v) for v in odd])


def mm(a, b, dims=((1,), (0,))):
    return lax.dot_general(a, b, (dims, ((), ())), precision=lax.Precision.HIGHEST, preferred_element_type=jnp.float32)


def factor(block, row, lane):
    m = jnp.where(lane - HALF == row, 1.0, block)
    tiles = [m[8 * t : 8 * t + 8] for t in range(8)]
    sub = lax.broadcasted_iota(jnp.int32, (8, LANES), 0)
    wide = lambda v: jnp.broadcast_to(v, (8, LANES))
    out = []
    for t in range(8):
        cols = {v: [wide(tiles[v][:, 8 * t + j : 8 * t + j + 1]) for j in range(8)] for v in range(t, 8)}
        c, d, q = cols[t], tiles[t], []
        for j in range(8):
            r = 1.0 / c[j][j : j + 1]
            out.append(d[j : j + 1] * lax.rsqrt(c[j][j : j + 1]))
            q.append(wide(d[j : j + 1] * r))
            below = jnp.where(sub > j, c[j], 0.0)
            d = d - below * q[j]
            for l in range(j + 1, 8):
                u = wide(c[l][j : j + 1] * r)
                c[l] = c[l] - below * u
                for v in range(t + 1, 8):
                    cols[v][l] = cols[v][l] - cols[v][j] * u
        for v in range(t + 1, 8):
            for j in range(8):
                tiles[v] = tiles[v] - cols[v][j] * q[j]
    return jnp.concatenate(out, axis=0)


def whiten_kernel(index_ref, damp_ref, g_ref, o_ref):
    packed = g_ref[0]
    for i in range(1, 8):
        packed = packed + g_ref[i]
    packed = packed / TOKENS
    row = lax.broadcasted_iota(jnp.int32, (HALF, LANES), 0)
    lane = lax.broadcasted_iota(jnp.int32, (HALF, LANES), 1)
    row32, lane32 = row[:32], lane[:32]
    low = packed[0:64]
    mid = packed[64:128]
    tail = packed[128:144]
    extra = jnp.broadcast_to(packed[144:145], (HALF, LANES))
    turned = rolled(mid, HALF)
    inside = lane < HALF
    upper00 = jnp.where((lane > row) & inside, turned, 0.0)
    lower11 = jnp.where((lane < row), turned, 0.0)
    diag11 = jnp.where(lane == row, turned, 0.0)
    folded = jnp.concatenate([tail, rolled(tail, HALF)], axis=0)
    h10 = jnp.where(lane32 < 32, folded, 0.0)
    fturn = rolled(folded, LANES - 32)
    hup = jnp.where((lane32 > row32) & (lane32 < 32), fturn, 0.0)
    hlow = jnp.where(lane32 < row32, fturn, 0.0)
    hdiag = jnp.where(lane32 == row32, fturn, 0.0)
    extra_turned = rolled(extra, HALF)
    diag00 = jnp.where(lane == row, extra_turned, 0.0)
    hdiag0 = jnp.where(lane32 == row32, extra[:32], 0.0)
    lower22 = jnp.concatenate([jnp.zeros((32, LANES), jnp.float32), h10 + jnp.where(lane32 >= 32, rolled(hlow, 32), 0.0)], axis=0)
    upper22 = jnp.concatenate([hup, jnp.zeros((32, LANES), jnp.float32)], axis=0)
    diag22 = jnp.concatenate([hdiag0, rolled(hdiag, 32)], axis=0)

    def flip(v):
        return jnp.concatenate([v.T[:HALF], jnp.zeros((HALF, HALF), jnp.float32)], axis=1)

    s00 = upper00 + flip(upper00) + diag00
    s11 = lower11 + flip(lower11) + diag11
    off22 = lower22 + upper22
    s22 = off22 + flip(off22) + diag22
    trace = jnp.sum(jnp.sum(diag00 + diag11 + diag22, axis=0, keepdims=True), axis=1, keepdims=True)
    scale = (1 << damp_ref[index_ref[0]]).astype(jnp.float32)
    damping = (trace / HD + 1e-6) / scale
    eye = jnp.where(lane == row, jnp.broadcast_to(damping, (HALF, LANES)), 0.0)
    s10 = mid[:, :HALF]
    s20, s21 = low[:, :HALF], low[:, HALF:]

    w0 = factor(s00 + eye, row, lane)[:, HALF:]
    u10 = mm(w0, s10, ((1,), (1,)))
    u20 = mm(w0, s20, ((1,), (1,)))
    pad = jnp.zeros((HALF, HALF), jnp.float32)
    r11 = s11 + eye - jnp.concatenate([mm(u10, u10, ((0,), (0,))), pad], axis=1)
    r21 = s21 - mm(u20, u10, ((0,), (0,)))
    w1 = factor(r11, row, lane)[:, HALF:]
    u21 = mm(w1, r21, ((1,), (1,)))
    gap = mm(u20, u20, ((0,), (0,))) + mm(u21, u21, ((0,), (0,)))
    r22 = s22 + eye - jnp.concatenate([gap, pad], axis=1)
    x10 = mm(u10, w0, ((0,), (0,)))
    w10 = -mm(w1, x10)
    x20 = mm(u20, w0, ((0,), (0,))) + mm(u21, w10, ((0,), (0,)))
    x21 = mm(u21, w1, ((0,), (0,)))
    w2 = factor(r22, row, lane)[:, HALF:]
    low_out = -mm(w2, jnp.concatenate([x20, x21], axis=1))
    for i in range(8):
        o_ref[i, 0:64] = jnp.concatenate([w0, w2], axis=1)
        o_ref[i, 64:128] = jnp.concatenate([w10, w1], axis=1)
        o_ref[i, 128:192] = low_out


def whiten(index, damp_exp, parts):
    smem = pl.BlockSpec(memory_space=pltpu.SMEM)
    return pl.pallas_call(
        whiten_kernel,
        in_specs=[smem, smem, WHOLE],
        out_specs=WHOLE,
        out_shape=pltpu.VMEM((8, OUT_ROWS, LANES), jnp.float32),
        compiler_params=params(8),
        name="whiten",
    )(index, damp_exp, on_chip(parts))


def spread_kernel(p_ref, o_ref):
    lane = lax.broadcasted_iota(jnp.int32, (HALF, LANES), 1)
    inside = lane < HALF
    for i in range(8):
        ends = p_ref[i, 0:64]
        o_ref[i, 0:64, 0:128] = jnp.where(inside, ends, 0.0)
        o_ref[i, 64:128, 0:128] = p_ref[i, 64:128]
        o_ref[i, 128:192, 0:128] = p_ref[i, 128:192]
        o_ref[i, 0:128, 128:192] = jnp.zeros((128, HALF), jnp.float32)
        o_ref[i, 128:192, 128:192] = rolled(ends, HALF)[:, :HALF]


def spread(packed):
    return pl.pallas_call(
        spread_kernel,
        grid=(1,),
        in_specs=[WHOLE],
        out_specs=pl.BlockSpec((8, HD, HD), lambda i: (0, 0, 0)),
        out_shape=jax.ShapeDtypeStruct((8, HD, HD), jnp.float32),
        compiler_params=params(8),
        name="spread",
    )(on_chip(packed))


def on_device(projected, weight_exp, damp_exp):
    dp, head = lax.axis_index("dp"), lax.axis_index("head")
    core = head % 2
    x, z, y_lo, y_hi = head // 4, dp % 4, dp // 4, head // 2 % 2
    y = 2 * y_hi + y_lo
    a = near(x) * 4 + near(y) * 2 + near(z)
    b = far(x) * 4 + far(y) * 2 + far(z)
    core, own_spot = core[None], jnp.where(core == 0, b, a)[None]
    theirs = [their_grams(projected, weight_exp, core, half) for half in range(2)]
    received = [lax.ppermute(part, DEVICES, partner_pairs()) for part in theirs]
    even = my_grams(projected, weight_exp, received[0], core, own_spot, 0).reshape(8, 4, ROWS, LANES)
    even = lax.all_to_all(even, DEVICES, 0, 0, tiled=True, axis_index_groups=cubes(0))
    odd = my_grams(projected, weight_exp, received[1], core, own_spot, 1)
    swapped = [odd[0]]
    for flip in range(1, 8):
        swapped.append(lax.ppermute(odd[flip], DEVICES, peers(flip)))
    even_sum = add_even(even)
    cube = add_odd(even_sum, swapped)
    parts = lax.all_to_all(cube, DEVICES, 0, 0, tiled=True, axis_index_groups=cubes(1))
    factors = whiten((head * 8 + dp)[None], damp_exp, parts)
    gathered = lax.all_to_all(factors, DEVICES, 0, 0, tiled=True, axis_index_groups=owner_groups())
    return spread(gathered)


def solution(mesh):
    return jax.shard_map(
        on_device,
        mesh=mesh,
        in_specs=(P(("dp", "head"), None), P(("dp", "head")), P()),
        out_specs=P("head", None, None),
        check_vma=False,
    )
```

profile of v0, /device:TPU:0, one launch (start us, length us, event | category | flops | bytes accessed | tf_op | source)
XLA Modules:
  0.0 102.2 jit_solution(16080575182055765771)
XLA Ops:
  0.0 6.3 %their_grams.2 = f32[32,152,128]{2,1,0:T(8,128)} custom-call(s32[1]{0:T(128)} %bitcast.1.core_ref, bf16[384,24576]{1,0:T(8,128)(2,1)} %x_ref.7, s32[384]{0:T(512)} %exp_ref.7), custom_call_target="tpu_custom_call" | custom-call | flops 905969664 | bytes 7500000 | tf_op jit(solution)/shard_map/their_grams/pallas_call | solution.py:148
  6.3 0.0 collective-permute-start
  6.3 4.9 %their_grams.3 = f32[32,152,128]{2,1,0:T(8,128)S(1)} custom-call(s32[1]{0:T(128)} %bitcast.1.core_ref, bf16[384,24576]{1,0:T(8,128)(2,1)} %x_ref.7, s32[384]{0:T(512)} %exp_ref.7), custom_call_target="tpu_custom_call" | custom-call | flops 905969664 | bytes 7500000 | tf_op jit(solution)/shard_map/their_grams/pallas_call | solution.py:148
  11.2 0.6 collective-permute-start.1
  11.8 0.0 collective-permute-done.received_ref
  11.8 7.2 %my_grams.2 = f32[32,152,128]{2,1,0:T(8,128)} custom-call(s32[1]{0:T(128)} %bitcast.1.core_ref, s32[1]{0:T(128)} %bitcast.2.spot_ref, bf16[384,24576]{1,0:T(8,128)(2,1)} %x_ref.7, s32[384]{0:T(512)} %exp_ref.7, f32[32,152,128]{2,1,0:T(8,128)} %collective-permute-done.received_ref), custom_call_target="tpu_custom_call" | custom-call | flops 905969664 | bytes 10000000 | tf_op jit(solution)/shard_map/my_grams/pallas_call | solution.py:211
  19.0 5.2 %all-to-all-start = ((f32[8,4,152,128]{3,2,1,0:T(8,128)}), f32[8,4,152,128]{3,2,1,0:T(8,128)}, u32[]{:S(2)}, u32[]{:S(2)}) async-start(f32[8,4,152,128]{3,2,1,0:T(8,128)} %bitcast.4), calls=%async_computation | async-start | bytes 4980736 | tf_op jit(solution)/shard_map/all_to_all | solution.py:419
  24.2 0.0 collective-permute-done.1.received_ref
  24.2 6.7 %my_grams.3 = (f32[4,152,128]{2,1,0:T(8,128)S(1)}, f32[4,152,128]{2,1,0:T(8,128)S(1)}, f32[4,152,128]{2,1,0:T(8,128)S(1)}, f32[4,152,128]{2,1,0:T(8,128)}, f32[4...) custom-call(s32[1]{0:T(128)} %bitcast.1.core_ref, ...), custom_call_target="tpu_custom_call" | custom-call | flops 905969664 | bytes 10000000 | tf_op jit(solution)/shard_map/my_grams/pallas_call | solution.py:211
  30.9 2.0 %collective-permute-start.2 = (f32[4,152,128]{2,1,0:T(8,128)S(1)}, f32[4,152,128]{2,1,0:T(8,128)S(1)}, u32[]{:S(2)}, u32[]{:S(2)}) collective-permute-start(f32[4,152,128]{2,1,0:T(8,128)S(1)} %get-tuple-element.14), channel_id=1, source_target_pairs={{0,16},{1,49},{2,18},{3,51},{4,20},{5,53},{6,22},{7,55},{8,24},{9,... | collective-permute-start | bytes 933896 | tf_op jit(solution)/shard_map/ppermute | solution.py:423
  33.0 1.4 %collective-permute-start.3 = (f32[4,152,128]{2,1,0:T(8,128)S(1)}, f32[4,152,128]{2,1,0:T(8,128)S(1)}, u32[]{:S(2)}, u32[]{:S(2)}) collective-permute-start(f32[4,152,128]{2,1,0:T(8,128)S(1)} %get-tuple-element.15), channel_id=1, source_target_pairs={{0,64},{1,67},{2,66},{3,65},{4,68},{5,71},{6,70},{7,69},{8,72},{9,... | collective-permute-start | bytes 933896 | tf_op jit(solution)/shard_map/ppermute | solution.py:423
  34.4 0.0 collective-permute-start.4
  34.4 2.0 %collective-permute-start.5 = (f32[4,152,128]{2,1,0:T(8,128)}, f32[4,152,128]{2,1,0:T(8,128)S(1)}, u32[]{:S(2)}, u32[]{:S(2)}) collective-permute-start(f32[4,152,128]{2,1,0:T(8,128)} %get-tuple-element.17), channel_id=1, source_target_pairs={{0,4},{1,13},{2,6},{3,15},{4,0},{5,9},{6,2},{7,11},{8,12},{9,5},{1... | collective-permute-start | bytes 933896 | tf_op jit(solution)/shard_map/ppermute | solution.py:423
  36.4 1.5 %collective-permute-start.6 = (f32[4,152,128]{2,1,0:T(8,128)S(1)}, f32[4,152,128]{2,1,0:T(8,128)S(1)}, u32[]{:S(2)}, u32[]{:S(2)}) collective-permute-start(f32[4,152,128]{2,1,0:T(8,128)S(1)} %get-tuple-element.18), channel_id=1, source_target_pairs={{0,20},{1,61},{2,22},{3,63},{4,16},{5,57},{6,18},{7,59},{8,28},{9,... | collective-permute-start | bytes 933896 | tf_op jit(solution)/shard_map/ppermute | solution.py:423
  37.9 6.8 %collective-permute-done.2.refs_1_ = f32[4,152,128]{2,1,0:T(8,128)S(1)} collective-permute-done((f32[4,152,128]{2,1,0:T(8,128)S(1)}, f32[4,152,128]{2,1,0:T(8,128)S(1)}, u32[]{:S(2)}, u32[]{:S(2)}) %collective-permute-start.2) | collective-permute-done | bytes 311328 | tf_op jit(solution)/shard_map/ppermute | solution.py:423
  44.7 2.4 %collective-permute-start.7 = (f32[4,152,128]{2,1,0:T(8,128)S(1)}, f32[4,152,128]{2,1,0:T(8,128)S(1)}, u32[]{:S(2)}, u32[]{:S(2)}) collective-permute-start(f32[4,152,128]{2,1,0:T(8,128)S(1)} %get-tuple-element.19), channel_id=1, source_target_pairs={{0,68},{1,79},{2,70},{3,77},{4,64},{5,75},{6,66},{7,73},{8,76},{9,... | collective-permute-start | bytes 933896 | tf_op jit(solution)/shard_map/ppermute | solution.py:423
  47.0 0.0 collective-permute-done.3.refs_2_
  47.1 0.5 collective-permute-start.8
  47.6 0.0 all-to-all-done.even_ref
  47.6 2.5 %add_even.1.even_ref = f32[4,152,128]{2,1,0:T(8,128)S(1)} custom-call(f32[8,4,152,128]{3,2,1,0:T(8,128)} %all-to-all-done.even_ref), custom_call_target="tpu_custom_call" | custom-call | flops 6000000 | bytes 3000000 | tf_op jit(solution)/shard_map/add_even/pallas_call | solution.py:239
  50.1 0.0 copy-start
  50.1 2.1 %collective-permute-done.4.refs_3_ = f32[4,152,128]{2,1,0:T(8,128)S(1)} collective-permute-done((f32[4,152,128]{2,1,0:T(8,128)}, f32[4,152,128]{2,1,0:T(8,128)S(1)}, u32[]{:S(2)}, u32[]{:S(2)}) %collective-permute-start.4) | collective-permute-done | bytes 311328 | tf_op jit(solution)/shard_map/ppermute | solution.py:423
  52.2 0.0 collective-permute-done.5.refs_4_
  52.2 0.1 collective-permute-done.6.refs_5_
  52.3 2.7 %collective-permute-done.7.refs_6_ = f32[4,152,128]{2,1,0:T(8,128)S(1)} collective-permute-done((f32[4,152,128]{2,1,0:T(8,128)S(1)}, f32[4,152,128]{2,1,0:T(8,128)S(1)}, u32[]{:S(2)}, u32[]{:S(2)}) %collective-permute-start.7) | collective-permute-done | bytes 311328 | tf_op jit(solution)/shard_map/ppermute | solution.py:423
  55.0 3.9 %collective-permute-done.8.refs_7_ = f32[4,152,128]{2,1,0:T(8,128)S(1)} collective-permute-done((f32[4,152,128]{2,1,0:T(8,128)S(1)}, f32[4,152,128]{2,1,0:T(8,128)S(1)}, u32[]{:S(2)}, u32[]{:S(2)}) %collective-permute-start.8) | collective-permute-done | bytes 311328 | tf_op jit(solution)/shard_map/ppermute | solution.py:423
  58.9 1.0 add_odd.1
  59.9 9.1 %all-to-all-start.1 = ((f32[8,152,128]{2,1,0:T(8,128)}), f32[8,152,128]{2,1,0:T(8,128)S(1)}, u32[]{:S(2)}, u32[]{:S(2)}) async-start(f32[8,152,128]{2,1,0:T(8,128)} %add_odd.1), calls=%async_computation.1 | async-start | bytes 1245184 | tf_op jit(solution)/shard_map/all_to_all | solution.py:426
  69.0 11.7 %all-to-all-done.1.g_ref = f32[8,152,128]{2,1,0:T(8,128)S(1)} async-done(((f32[8,152,128]{2,1,0:T(8,128)}), f32[8,152,128]{2,1,0:T(8,128)S(1)}, u32[]{:S(2)}, u32[]{:S(2)}) %all-to-all-start.1) | async-done | bytes 622624 | tf_op jit(solution)/shard_map/all_to_all | solution.py:426
  80.7 6.6 %whiten.1 = f32[8,192,128]{2,1,0:T(8,128)S(1)} custom-call(s32[1]{0:T(128)} %bitcast.index_ref, s32[128]{0:T(128)S(1)} %copy-done, f32[8,152,128]{2,1,0:T(8,128)S(1)} %all-to-all-done.1.g_ref), custom_call_target="tpu_custom_call" | custom-call | tf_op jit(solution)/shard_map/whiten/pallas_call | solution.py:374
  87.3 13.6 %all_to_all.15.p_ref = f32[8,192,128]{2,1,0:T(8,128)S(1)} all-to-all(f32[8,192,128]{2,1,0:T(8,128)S(1)} %whiten.1), channel_id=1, replica_groups={{0,16,32,48,64,80,96,112},{1,17,33,49,65,81,97,113},{2,18,34,50,66,82,9..., dimensions={0} | all-to-all | bytes 1572864 | tf_op jit(solution)/shard_map/all_to_all | solution.py:428
  100.9 1.3 %spread.1 = f32[8,192,192]{2,1,0:T(8,128)} custom-call(f32[8,192,128]{2,1,0:T(8,128)S(1)} %all_to_all.15.p_ref), custom_call_target="tpu_custom_call" | custom-call | tf_op jit(solution)/shard_map/spread/pallas_call | solution.py:397
  (1 shorter events, 0.0 us)
Async XLA Ops:
  6.3 5.5 %collective-permute-start = (f32[32,152,128]{2,1,0:T(8,128)}, f32[32,152,128]{2,1,0:T(8,128)}, u32[]{:S(2)}, u32[]{:S(2)}) collective-permute-start(f32[32,152,128]{2,1,0:T(8,128)} %their_grams.2), channel_id=1, source_target_pairs={{0,1},{1,0},{2,3},{3,2},{4,5},{5,4},{6,7},{7,6},{8,9},{9,8},{10,11... | collective-permute-start | bytes 7471112 | tf_op jit(solution)/shard_map/ppermute | solution.py:417
  11.2 13.0 %collective-permute-start.1 = (f32[32,152,128]{2,1,0:T(8,128)S(1)}, f32[32,152,128]{2,1,0:T(8,128)}, u32[]{:S(2)}, u32[]{:S(2)}) collective-permute-start(f32[32,152,128]{2,1,0:T(8,128)S(1)} %their_grams.3), channel_id=1, source_target_pairs={{0,1},{1,0},{2,3},{3,2},{4,5},{5,4},{6,7},{7,6},{8,9},{9,8},{10,11... | collective-permute-start | bytes 7471112 | tf_op jit(solution)/shard_map/ppermute | solution.py:417
  19.0 28.6 %all-to-all-start = ((f32[8,4,152,128]{3,2,1,0:T(8,128)}), f32[8,4,152,128]{3,2,1,0:T(8,128)}, u32[]{:S(2)}, u32[]{:S(2)}) async-start(f32[8,4,152,128]{3,2,1,0:T(8,128)} %bitcast.4), calls=%async_computation | async-start | bytes 4980736 | tf_op jit(solution)/shard_map/all_to_all | solution.py:419
  30.9 13.7 %collective-permute-start.2 = (f32[4,152,128]{2,1,0:T(8,128)S(1)}, f32[4,152,128]{2,1,0:T(8,128)S(1)}, u32[]{:S(2)}, u32[]{:S(2)}) collective-permute-start(f32[4,152,128]{2,1,0:T(8,128)S(1)} %get-tuple-element.14), channel_id=1, source_target_pairs={{0,16},{1,49},{2,18},{3,51},{4,20},{5,53},{6,22},{7,55},{8,24},{9,... | collective-permute-start | bytes 933896 | tf_op jit(solution)/shard_map/ppermute | solution.py:423
  33.0 14.1 %collective-permute-start.3 = (f32[4,152,128]{2,1,0:T(8,128)S(1)}, f32[4,152,128]{2,1,0:T(8,128)S(1)}, u32[]{:S(2)}, u32[]{:S(2)}) collective-permute-start(f32[4,152,128]{2,1,0:T(8,128)S(1)} %get-tuple-element.15), channel_id=1, source_target_pairs={{0,64},{1,67},{2,66},{3,65},{4,68},{5,71},{6,70},{7,69},{8,72},{9,... | collective-permute-start | bytes 933896 | tf_op jit(solution)/shard_map/ppermute | solution.py:423
  34.4 17.8 %collective-permute-start.4 = (f32[4,152,128]{2,1,0:T(8,128)}, f32[4,152,128]{2,1,0:T(8,128)S(1)}, u32[]{:S(2)}, u32[]{:S(2)}) collective-permute-start(f32[4,152,128]{2,1,0:T(8,128)} %get-tuple-element.16), channel_id=1, source_target_pairs={{0,80},{1,115},{2,82},{3,113},{4,84},{5,119},{6,86},{7,117},{8,88}... | collective-permute-start | bytes 933896 | tf_op jit(solution)/shard_map/ppermute | solution.py:423
  34.4 17.8 %collective-permute-start.5 = (f32[4,152,128]{2,1,0:T(8,128)}, f32[4,152,128]{2,1,0:T(8,128)S(1)}, u32[]{:S(2)}, u32[]{:S(2)}) collective-permute-start(f32[4,152,128]{2,1,0:T(8,128)} %get-tuple-element.17), channel_id=1, source_target_pairs={{0,4},{1,13},{2,6},{3,15},{4,0},{5,9},{6,2},{7,11},{8,12},{9,5},{1... | collective-permute-start | bytes 933896 | tf_op jit(solution)/shard_map/ppermute | solution.py:423
  36.4 15.9 %collective-permute-start.6 = (f32[4,152,128]{2,1,0:T(8,128)S(1)}, f32[4,152,128]{2,1,0:T(8,128)S(1)}, u32[]{:S(2)}, u32[]{:S(2)}) collective-permute-start(f32[4,152,128]{2,1,0:T(8,128)S(1)} %get-tuple-element.18), channel_id=1, source_target_pairs={{0,20},{1,61},{2,22},{3,63},{4,16},{5,57},{6,18},{7,59},{8,28},{9,... | collective-permute-start | bytes 933896 | tf_op jit(solution)/shard_map/ppermute | solution.py:423
  44.7 10.3 %collective-permute-start.7 = (f32[4,152,128]{2,1,0:T(8,128)S(1)}, f32[4,152,128]{2,1,0:T(8,128)S(1)}, u32[]{:S(2)}, u32[]{:S(2)}) collective-permute-start(f32[4,152,128]{2,1,0:T(8,128)S(1)} %get-tuple-element.19), channel_id=1, source_target_pairs={{0,68},{1,79},{2,70},{3,77},{4,64},{5,75},{6,66},{7,73},{8,76},{9,... | collective-permute-start | bytes 933896 | tf_op jit(solution)/shard_map/ppermute | solution.py:423
  47.1 11.9 %collective-permute-start.8 = (f32[4,152,128]{2,1,0:T(8,128)S(1)}, f32[4,152,128]{2,1,0:T(8,128)S(1)}, u32[]{:S(2)}, u32[]{:S(2)}) collective-permute-start(f32[4,152,128]{2,1,0:T(8,128)S(1)} %get-tuple-element.20), channel_id=1, source_target_pairs={{0,84},{1,127},{2,86},{3,125},{4,80},{5,123},{6,82},{7,121},{8,92}... | collective-permute-start | bytes 933896 | tf_op jit(solution)/shard_map/ppermute | solution.py:423
  50.1 30.7 %copy-start = (s32[128]{0:T(128)S(1)}, s32[128]{0:T(128)}, u32[]{:S(2)}) copy-start(s32[128]{0:T(128)} %damp_ref.1) | copy-start | bytes 1540
  59.9 20.8 %all-to-all-start.1 = ((f32[8,152,128]{2,1,0:T(8,128)}), f32[8,152,128]{2,1,0:T(8,128)S(1)}, u32[]{:S(2)}, u32[]{:S(2)}) async-start(f32[8,152,128]{2,1,0:T(8,128)} %add_odd.1), calls=%async_computation.1 | async-start | bytes 1245184 | tf_op jit(solution)/shard_map/all_to_all | solution.py:426
where the time goes:
time: 103 us; the launch traced here: 102 us
  Pallas kernels  36.4 us (35%)
  waiting for transfers between devices  27.3 us (27%)
  starting transfers between devices  24.8 us (24%)
  blocking collectives  13.6 us (13%)
    ppermute x7, waiting for transfers between devices, on_device(): swapped.append(lax.ppermute(odd[flip], DEVICES, peers(flip)))  15.6 us
    pallas_call x2, Pallas kernels, my_grams(): pl.pallas_call(kernel, grid_spec=pltpu.PrefetchScalarGridSpec(num_scalar_...  13.9 us
    all_to_all x1, blocking collectives, on_device(): lax.all_to_all(factors, DEVICES, 0, 0, tiled=True, axis_index_groups=owne...  13.6 us
    all_to_all x1, waiting for transfers between devices, on_device(): lax.all_to_all(cube, DEVICES, 0, 0, tiled=True, axis_index_groups=cubes(1))  11.7 us
    pallas_call x2, Pallas kernels, their_grams(): pl.pallas_call(their_grams_kernel, grid_spec=pltpu.PrefetchScalarGridSpec...  11.2 us
    ppermute x7, starting transfers between devices, on_device(): swapped.append(lax.ppermute(odd[flip], DEVICES, peers(flip)))  9.87 us
    all_to_all x1, starting transfers between devices, on_device(): lax.all_to_all(cube, DEVICES, 0, 0, tiled=True, axis_index_groups=cubes(1))  9.11 us
    pallas_call x1, Pallas kernels, whiten(): pl.pallas_call(whiten_kernel, in_specs=[smem, smem, WHOLE], out_specs=WHO...  6.57 us
  transfers between devices with their start and end apart: 11, of which 6 were waited for; matrix products, arithmetic and copies ran while one was open for 0% of the time, Pallas kernels for 21%

commit v1 on v0

--- a/solution.py
+++ b/solution.py
@@ -9,8 +9,11 @@
 HALF = 64
 LANES = 128
 ROWS = 152
-OUT_ROWS = 192
+BODY = 144
+BLOCK_ROWS = 8 * BODY + 8
+SLOT_ROWS = 4 * BODY + 8
 TOKENS = 49152
+PANEL = 2
 DEVICES = ("dp", "head")
 
 
@@ -66,7 +69,7 @@
     y = 2 * y_hi + y_lo
     a, a_rest = near(x) * 4 + near(y) * 2 + near(z), near(y) * 2 + near(z)
     b, b_rest = far(x) * 4 + far(y) * 2 + far(z), far(y) * 2 + far(z)
-    return jnp.where(core == 0, b * 4 + a_rest, a * 4 + b_rest)
+    return jnp.where(core == 0, b, a), jnp.where(core == 0, a_rest, b_rest)
 
 
 def on_chip(v):
@@ -88,14 +91,13 @@
     return pltpu.roll(v, by, 1)
 
 
-def block_grams(x_ref, w_ref, put):
+def block_grams(x_ref, w_ref, put, put_diag):
     w = w_ref[...]
     w3 = jnp.concatenate([w, w, w], axis=1)
     row = lax.broadcasted_iota(jnp.int32, (HALF, LANES), 0)
     lane = lax.broadcasted_iota(jnp.int32, (HALF, LANES), 1)
     row32, lane32 = row[:32], lane[:32]
     row16, lane16 = row[:16], lane[:16]
-    row8 = row[:8]
     contract = (((0,), (0,)), ((), ()))
 
     def finish(index, low, mid, first, last, at):
@@ -111,7 +113,7 @@
         diag = jnp.sum(jnp.where(lane - HALF == row, first, 0.0), axis=0, keepdims=True)
         small = jnp.sum(jnp.where(lane32 - at == row32, last[:32], 0.0), axis=0, keepdims=True)
         diag = jnp.broadcast_to(diag, (8, LANES)) + moved(jnp.broadcast_to(small, (8, LANES)), 0)
-        put(index, 144, jnp.where(row8 == 0, diag, 0.0))
+        put_diag(index, diag[:1])
 
     for pair in range(4):
         x = x_ref[:, 384 * pair : 384 * (pair + 1)]
@@ -131,16 +133,21 @@
 
 
 def their_grams_kernel(core_ref, x_ref, exp_ref, o_ref, w_ref):
-    @pl.when(pl.program_id(0) == 0)
+    i = pl.program_id(0)
+
+    @pl.when(i == 0)
     def _():
         spread_weights(exp_ref, w_ref)
 
-    i = pl.program_id(0)
+    base = BLOCK_ROWS * i if o_ref.shape[0] > BLOCK_ROWS else 0
 
     def put(index, start, rows):
-        o_ref[8 * i + index, start : start + rows.shape[0]] = rows
-
-    block_grams(x_ref, w_ref, put)
+        o_ref[pl.ds(pl.multiple_of(base + BODY * index + start, 8), rows.shape[0])] = rows
+
+    def put_diag(index, diag):
+        o_ref[pl.ds(pl.multiple_of(base + 8 * BODY, 8) + index, 1)] = diag
+
+    block_grams(x_ref, w_ref, put, put_diag)
 
 
 def their_grams(projected, weight_exp, core, half):
@@ -154,35 +161,53 @@
                 pl.BlockSpec((tokens, 8 * HD), lambda i, core: (0, 2 * chunk_block(half, i) + 1 - core[0])),
                 pl.BlockSpec((tokens,), lambda i, core: (0,)),
             ],
-            out_specs=WHOLE,
+            out_specs=WHOLE if half else pl.BlockSpec((BLOCK_ROWS, LANES), lambda i, core: (i, 0)),
             scratch_shapes=[pltpu.VMEM((tokens, LANES), jnp.bfloat16)],
         ),
-        out_shape=pltpu.VMEM((32, ROWS, LANES), jnp.float32),
+        out_shape=(pltpu.VMEM if half else pltpu.HBM)((4 * BLOCK_ROWS, LANES), jnp.float32),
         compiler_params=params(12, dimension_semantics=("arbitrary",)),
         cost_estimate=pl.CostEstimate(flops=tokens * 64 * HD * HD, bytes_accessed=7_500_000, transcendentals=0),
         name="their_grams",
     )(core, off_chip(projected), off_chip(weight_exp))
 
 
-def my_even_kernel(core_ref, spot_ref, x_ref, exp_ref, received_ref, o_ref, w_ref):
-    fill_slots(0, core_ref, x_ref, exp_ref, received_ref, o_ref, w_ref)
-
-
-def fill_slots(half, core_ref, x_ref, exp_ref, received_ref, o_ref, w_ref):
+def fill_slots(half, core_ref, x_ref, exp_ref, received_ref, all_ref, w_ref):
     i = pl.program_id(0)
 
     @pl.when(i == 0)
     def _():
         spread_weights(exp_ref, w_ref)
+        for slot in range(8):
+            all_ref[slot, SLOT_ROWS - 8 :] = jnp.zeros((8, LANES), jnp.float32)
 
     block = chunk_block(half, i)
-    slots = [spot(block, inner, core_ref[0]) for inner in range(8)]
+    spots = [spot(block, inner, core_ref[0]) for inner in range(8)]
 
     def put(index, start, rows):
+        slot, rest = spots[index]
         size = rows.shape[0]
-        o_ref[slots[index], start : start + size] = rows + received_ref[8 * i + index, start : start + size]
-
-    block_grams(x_ref, w_ref, put)
+        at = pl.multiple_of(BODY * rest + start, 8)
+        all_ref[slot, pl.ds(at, size)] = rows + received_ref[BODY * index + start : BODY * index + start + size]
+
+    def put_diag(index, diag):
+        slot, rest = spots[index]
+        all_ref[slot, pl.ds(4 * BODY + rest, 1)] = diag + received_ref[8 * BODY + index : 8 * BODY + index + 1]
+
+    block_grams(x_ref, w_ref, put, put_diag)
+    return spots
+
+
+def my_even_kernel(core_ref, spot_ref, x_ref, exp_ref, received_ref, o_ref, w_ref, all_ref, sem):
+    spots = fill_slots(0, core_ref, x_ref, exp_ref, received_ref, all_ref, w_ref)
+    for slot, rest in spots:
+        rows = pl.ds(pl.multiple_of(BODY * rest, 8), BODY)
+        pltpu.make_async_copy(all_ref.at[slot, rows], o_ref.at[slot, rows], sem).start()
+
+    @pl.when(pl.program_id(0) == pl.num_programs(0) - 1)
+    def _():
+        rows = pl.ds(4 * BODY, 8)
+        pltpu.make_async_copy(all_ref.at[:, rows], o_ref.at[:, rows], sem).start()
+        pltpu.make_async_copy(all_ref, o_ref, sem).wait()
 
 
 def my_odd_kernel(core_ref, spot_ref, x_ref, exp_ref, received_ref, *refs):
@@ -192,22 +217,19 @@
     @pl.when(pl.program_id(0) == pl.num_programs(0) - 1)
     def _():
         for flip in range(8):
-            slot = spot_ref[0] ^ flip
-            for i in range(4):
-                outs[flip][i] = all_ref[slot * 4 + i]
+            outs[flip][...] = all_ref[spot_ref[0] ^ flip]
 
 
 def my_grams(projected, weight_exp, received, core, own_spot, half):
     tokens = projected.shape[0]
-
-    scratch = [pltpu.VMEM((tokens, LANES), jnp.bfloat16)]
+    scratch = [pltpu.VMEM((tokens, LANES), jnp.bfloat16), pltpu.VMEM((8, SLOT_ROWS, LANES), jnp.float32)]
     if half:
         kernel, outs = my_odd_kernel, [WHOLE] * 8
-        shapes = [pltpu.VMEM((4, ROWS, LANES), jnp.float32)] * 8
-        scratch.append(pltpu.VMEM((32, ROWS, LANES), jnp.float32))
+        shapes = [pltpu.VMEM((SLOT_ROWS, LANES), jnp.float32)] * 8
     else:
-        kernel, outs = my_even_kernel, WHOLE
-        shapes = pltpu.HBM((32, ROWS, LANES), jnp.float32)
+        kernel, outs = my_even_kernel, pl.BlockSpec(memory_space=pl.ANY)
+        shapes = pltpu.HBM((8, SLOT_ROWS, LANES), jnp.float32)
+        scratch.append(pltpu.SemaphoreType.DMA(()))
     return pl.pallas_call(
         kernel,
         grid_spec=pltpu.PrefetchScalarGridSpec(
@@ -216,7 +238,7 @@
             in_specs=[
                 pl.BlockSpec((tokens, 8 * HD), lambda i, core, spot: (0, 2 * chunk_block(half, i) + core[0])),
                 pl.BlockSpec((tokens,), lambda i, core, spot: (0,)),
-                WHOLE,
+                pl.BlockSpec((BLOCK_ROWS, LANES), lambda i, core, spot: (i, 0)),
             ],
             out_specs=outs,
             scratch_shapes=scratch,
@@ -225,24 +247,28 @@
         compiler_params=params(16, dimension_semantics=("arbitrary",)),
         cost_estimate=pl.CostEstimate(flops=tokens * 64 * HD * HD, bytes_accessed=10_000_000, transcendentals=0),
         name="my_grams",
-    )(core, own_spot, off_chip(projected), off_chip(weight_exp), on_chip(received))
+    )(core, own_spot, off_chip(projected), off_chip(weight_exp), off_chip(received))
 
 
 def even_kernel(even_ref, o_ref):
-    total = even_ref[0, 0]
-    for k in range(1, 8):
-        total = total + even_ref[k, 0]
-    o_ref[pl.program_id(0)] = total
+    def one(i, carry):
+        rows = pl.ds(pl.multiple_of(8 * i, 8), 8)
+        total = even_ref[0, rows]
+        for k in range(1, 8):
+            total = total + even_ref[k, rows]
+        o_ref[rows] = total
+        return carry
+
+    lax.fori_loop(0, SLOT_ROWS // 8, one, 0, unroll=8)
 
 
 def add_even(even):
     return pl.pallas_call(
         even_kernel,
-        grid=(4,),
-        in_specs=[pl.BlockSpec((8, 1, ROWS, LANES), lambda i: (0, i, 0, 0))],
+        in_specs=[WHOLE],
         out_specs=WHOLE,
-        out_shape=pltpu.VMEM((4, ROWS, LANES), jnp.float32),
-        compiler_params=params(8, dimension_semantics=("arbitrary",)),
+        out_shape=pltpu.VMEM((SLOT_ROWS, LANES), jnp.float32),
+        compiler_params=params(8),
         cost_estimate=pl.CostEstimate(flops=6_000_000, bytes_accessed=3_000_000, transcendentals=0),
         name="add_even",
     )(off_chip(even))
@@ -250,16 +276,20 @@
 
 def odd_kernel(even_ref, *refs):
     odd_refs, o_ref = refs[:8], refs[8]
-
-    def one(i, carry):
-        o_ref[i] = even_ref[i]
-        total = odd_refs[0][i]
+    for i in range(4):
+        rows = slice(BODY * i, BODY * (i + 1))
+        o_ref[i, :BODY] = even_ref[rows]
+        total = odd_refs[0][rows]
         for k in range(1, 8):
-            total = total + odd_refs[k][i]
-        o_ref[4 + i] = total
-        return carry
-
-    lax.fori_loop(0, 4, one, 0)
+            total = total + odd_refs[k][rows]
+        o_ref[4 + i, :BODY] = total
+    last = slice(4 * BODY, SLOT_ROWS)
+    total = odd_refs[0][last]
+    for k in range(1, 8):
+        total = total + odd_refs[k][last]
+    for half, diags in enumerate((even_ref[last], total)):
+        for i in range(4):
+            o_ref[4 * half + i, BODY:] = jnp.broadcast_to(diags[i : i + 1], (8, LANES))
 
 
 def add_odd(even_sum, odd):
@@ -283,22 +313,25 @@
     sub = lax.broadcasted_iota(jnp.int32, (8, LANES), 0)
     wide = lambda v: jnp.broadcast_to(v, (8, LANES))
     out = []
-    for t in range(8):
-        cols = {v: [wide(tiles[v][:, 8 * t + j : 8 * t + j + 1]) for j in range(8)] for v in range(t, 8)}
-        c, d, q = cols[t], tiles[t], []
-        for j in range(8):
-            r = 1.0 / c[j][j : j + 1]
-            out.append(d[j : j + 1] * lax.rsqrt(c[j][j : j + 1]))
-            q.append(wide(d[j : j + 1] * r))
-            below = jnp.where(sub > j, c[j], 0.0)
-            d = d - below * q[j]
-            for l in range(j + 1, 8):
-                u = wide(c[l][j : j + 1] * r)
-                c[l] = c[l] - below * u
-                for v in range(t + 1, 8):
-                    cols[v][l] = cols[v][l] - cols[v][j] * u
-        for v in range(t + 1, 8):
-            for j in range(8):
+    for t in range(0, 8, PANEL):
+        size = 8 * PANEL
+        cols = {v: [wide(tiles[v][:, 8 * t + j : 8 * t + j + 1]) for j in range(size)] for v in range(t, 8)}
+        q = []
+        for j in range(size):
+            own, k = t + j // 8, j % 8
+            c, d = cols[own], tiles[own]
+            r = 1.0 / c[j][k : k + 1]
+            out.append(d[k : k + 1] * lax.rsqrt(c[j][k : k + 1]))
+            q.append(wide(d[k : k + 1] * r))
+            u = {l: wide(c[l][k : k + 1] * r) for l in range(j + 1, size)}
+            for v in range(own, 8):
+                part = jnp.where(sub > k, cols[v][j], 0.0) if v == own else cols[v][j]
+                if v < t + PANEL:
+                    tiles[v] = tiles[v] - part * q[j]
+                for l in range(j + 1, size):
+                    cols[v][l] = cols[v][l] - part * u[l]
+        for v in range(t + PANEL, 8):
+            for j in range(size):
                 tiles[v] = tiles[v] - cols[v][j] * q[j]
     return jnp.concatenate(out, axis=0)
 
@@ -363,10 +396,25 @@
     x21 = mm(u21, w1, ((0,), (0,)))
     w2 = factor(r22, row, lane)[:, HALF:]
     low_out = -mm(w2, jnp.concatenate([x20, x21], axis=1))
+
+    def twice(v):
+        return jnp.concatenate([v, v], axis=1)
+
+    turned0 = twice(w0).T
+    turned0 = jnp.concatenate([turned0[:HALF], turned0[HALF:]], axis=1)
+    middle = jnp.where(lane - HALF > row, turned0, jnp.concatenate([w10, w1], axis=1))
+    w2_wide = twice(w2)
+    corner = w2_wide[:32]
+    corner = jnp.concatenate([corner] * 4, axis=0).T[:32]
+    tri = jnp.where((lane32 & 63) - 32 > row32, corner, w2_wide[32:])
+    tri = jnp.where(lane[:16] < HALF, tri[:16], tri[16:])
+    diag = jnp.sum(jnp.where(lane == row, twice(w0), 0.0), axis=0, keepdims=True)
+    diag += jnp.sum(jnp.where(lane32 - HALF == row32, w2_wide[:32], 0.0), axis=0, keepdims=True)
     for i in range(8):
-        o_ref[i, 0:64] = jnp.concatenate([w0, w2], axis=1)
-        o_ref[i, 64:128] = jnp.concatenate([w10, w1], axis=1)
-        o_ref[i, 128:192] = low_out
+        o_ref[i, 0:64] = low_out
+        o_ref[i, 64:128] = middle
+        o_ref[i, 128:144] = tri
+        o_ref[i, 144:152] = jnp.broadcast_to(diag, (8, LANES))
 
 
 def whiten(index, damp_exp, parts):
@@ -375,22 +423,33 @@
         whiten_kernel,
         in_specs=[smem, smem, WHOLE],
         out_specs=WHOLE,
-        out_shape=pltpu.VMEM((8, OUT_ROWS, LANES), jnp.float32),
+        out_shape=pltpu.VMEM((8, ROWS, LANES), jnp.float32),
         compiler_params=params(8),
         name="whiten",
     )(index, damp_exp, on_chip(parts))
 
 
 def spread_kernel(p_ref, o_ref):
+    row = lax.broadcasted_iota(jnp.int32, (HALF, LANES), 0)
     lane = lax.broadcasted_iota(jnp.int32, (HALF, LANES), 1)
-    inside = lane < HALF
+    row32, lane32 = row[:32], lane[:32]
     for i in range(8):
-        ends = p_ref[i, 0:64]
-        o_ref[i, 0:64, 0:128] = jnp.where(inside, ends, 0.0)
-        o_ref[i, 64:128, 0:128] = p_ref[i, 64:128]
-        o_ref[i, 128:192, 0:128] = p_ref[i, 128:192]
+        middle = p_ref[i, 64:128]
+        tail = p_ref[i, 128:144]
+        diag = p_ref[i, 144:145]
+        turned = jnp.concatenate([middle, middle], axis=0).T[HALF:]
+        first = jnp.where(lane < row, turned, jnp.where(lane == row, diag, 0.0))
+        o_ref[i, 0:64, 0:128] = first
+        o_ref[i, 64:128, 0:128] = jnp.where(lane - HALF <= row, middle, 0.0)
+        o_ref[i, 128:192, 0:128] = p_ref[i, 0:64]
         o_ref[i, 0:128, 128:192] = jnp.zeros((128, HALF), jnp.float32)
-        o_ref[i, 128:192, 128:192] = rolled(ends, HALF)[:, :HALF]
+        lower = jnp.concatenate([tail, rolled(tail, HALF)], axis=0)
+        corner = jnp.concatenate([lower] * 4, axis=0).T[32:64]
+        corner_diag = rolled(jnp.broadcast_to(diag, (32, LANES)), HALF)
+        top = jnp.where(lane32 < row32, corner, jnp.where(lane32 == row32, corner_diag, 0.0))
+        bottom = jnp.where(lane32 - 32 <= row32, lower, 0.0)
+        o_ref[i, 128:160, 128:192] = top[:, :HALF]
+        o_ref[i, 160:192, 128:192] = bottom[:, :HALF]
 
 
 def spread(packed):
@@ -415,7 +474,7 @@
     core, own_spot = core[None], jnp.where(core == 0, b, a)[None]
     theirs = [their_grams(projected, weight_exp, core, half) for half in range(2)]
     received = [lax.ppermute(part, DEVICES, partner_pairs()) for part in theirs]
-    even = my_grams(projected, weight_exp, received[0], core, own_spot, 0).reshape(8, 4, ROWS, LANES)
+    even = my_grams(projected, weight_exp, received[0], core, own_spot, 0)
     even = lax.all_to_all(even, DEVICES, 0, 0, tiled=True, axis_index_groups=cubes(0))
     odd = my_grams(projected, weight_exp, received[1], core, own_spot, 1)
     swapped = [odd[0]]

time: 103 us -> 97.8 us (0.950)
  Pallas kernels: 36.4 us -> 33.5 us
  blocking collectives: 13.6 us -> 11.6 us
    all_to_all x1, blocking collectives: 13.6 us -> 11.6 us  [on_device(): lax.all_to_all(factors, DEVICES, 0, 0, tiled=True, axis_index_groups=owne...]
    pallas_call x2, Pallas kernels: 13.9 us -> 12.6 us  [my_grams(): pl.pallas_call(kernel, grid_spec=pltpu.PrefetchScalarGridSpec(num_scalar_...]
  transfers between devices with their start and end apart: 11 -> 11, of which waited for: 6 -> 6; matrix products, arithmetic and copies ran while one was open for 0% -> 0% of each run, Pallas kernels for 21% -> 20%
where the time goes in v1:
time: 97.8 us; the launch traced here: 97.3 us
  Pallas kernels  33.5 us (34%)
  waiting for transfers between devices  27.2 us (28%)
  starting transfers between devices  24.8 us (25%)
  blocking collectives  11.6 us (12%)
    ppermute x7, waiting for transfers between devices, on_device(): swapped.append(lax.ppermute(odd[flip], DEVICES, peers(flip)))  15.5 us
    pallas_call x2, Pallas kernels, my_grams(): pl.pallas_call(kernel, grid_spec=pltpu.PrefetchScalarGridSpec(num_scalar_...  12.6 us
    all_to_all x1, waiting for transfers between devices, on_device(): lax.all_to_all(cube, DEVICES, 0, 0, tiled=True, axis_index_groups=cubes(1))  11.7 us
    all_to_all x1, blocking collectives, on_device(): lax.all_to_all(factors, DEVICES, 0, 0, tiled=True, axis_index_groups=owne...  11.6 us
    pallas_call x2, Pallas kernels, their_grams(): pl.pallas_call(their_grams_kernel, grid_spec=pltpu.PrefetchScalarGridSpec...  10.8 us
    ppermute x7, starting transfers between devices, on_device(): swapped.append(lax.ppermute(odd[flip], DEVICES, peers(flip)))  9.85 us
    all_to_all x1, starting transfers between devices, on_device(): lax.all_to_all(cube, DEVICES, 0, 0, tiled=True, axis_index_groups=cubes(1))  9.08 us
    pallas_call x1, Pallas kernels, whiten(): pl.pallas_call(whiten_kernel, in_specs=[smem, smem, WHOLE], out_specs=WHO...  5.78 us
  transfers between devices with their start and end apart: 11, of which 6 were waited for; matrix products, arithmetic and copies ran while one was open for 0% of the time, Pallas kernels for 20%

profile of v1, /device:TPU:0, one launch (start us, length us, event | category | flops | bytes accessed | tf_op | source)
XLA Modules:
  0.0 97.3 jit_solution(1777277220680540012)
XLA Ops:
  0.0 5.9 %their_grams.2 = f32[4640,128]{1,0:T(8,128)} custom-call(s32[1]{0:T(128)} %bitcast.1.core_ref, bf16[384,24576]{1,0:T(8,128)(2,1)} %x_ref.7, s32[384]{0:T(512)} %exp_ref.7), custom_call_target="tpu_custom_call" | custom-call | flops 905969664 | bytes 7500000 | tf_op jit(solution)/shard_map/their_grams/pallas_call | solution.py:155
  5.9 0.0 collective-permute-start
  5.9 4.9 %their_grams.3 = f32[4640,128]{1,0:T(8,128)S(1)} custom-call(s32[1]{0:T(128)} %bitcast.1.core_ref, bf16[384,24576]{1,0:T(8,128)(2,1)} %x_ref.7, s32[384]{0:T(512)} %exp_ref.7), custom_call_target="tpu_custom_call" | custom-call | flops 905969664 | bytes 7500000 | tf_op jit(solution)/shard_map/their_grams/pallas_call | solution.py:155
  10.8 0.6 collective-permute-start.1
  11.4 0.0 collective-permute-done.received_ref
  11.4 6.3 %my_grams.2 = f32[8,584,128]{2,1,0:T(8,128)} custom-call(s32[1]{0:T(128)} %bitcast.1.core_ref, s32[1]{0:T(128)} %bitcast.2.spot_ref, bf16[384,24576]{1,0:T(8,128)(2,1)} %x_ref.7, s32[384]{0:T(512)} %exp_ref.7, f32[4640,128]{1,0:T(8,128)} %collective-permute-done.received_ref), custom_call_target="tpu_custom_call" | custom-call | flops 905969664 | bytes 10000000 | tf_op jit(solution)/shard_map/my_grams/pallas_call | solution.py:233
  17.7 5.3 %all-to-all-start = ((f32[8,584,128]{2,1,0:T(8,128)}), f32[8,584,128]{2,1,0:T(8,128)}, u32[]{:S(2)}, u32[]{:S(2)}) async-start(f32[8,584,128]{2,1,0:T(8,128)} %my_grams.2), calls=%async_computation | async-start | bytes 4784128 | tf_op jit(solution)/shard_map/all_to_all | solution.py:478
  23.0 0.0 collective-permute-done.1.received_ref
  23.0 6.2 %my_grams.3 = (f32[584,128]{1,0:T(8,128)S(1)}, f32[584,128]{1,0:T(8,128)S(1)}, f32[584,128]{1,0:T(8,128)S(1)}, f32[584,128]{1,0:T(8,128)}, f32[584,128]{1,0:T(8,...) custom-call(s32[1]{0:T(128)} %bitcast.1.core_ref, s32[1]{0:T(128)} %bitcast.2.spot_ref, ...), custom_call_target="tpu_custom_call" | custom-call | flops 905969664 | bytes 10000000 | tf_op jit(solution)/shard_map/my_grams/pallas_call | solution.py:233
  29.2 2.0 %collective-permute-start.2 = (f32[584,128]{1,0:T(8,128)S(1)}, f32[584,128]{1,0:T(8,128)S(1)}, u32[]{:S(2)}, u32[]{:S(2)}) collective-permute-start(f32[584,128]{1,0:T(8,128)S(1)} %get-tuple-element.14), channel_id=1, source_target_pairs={{0,16},{1,49},{2,18},{3,51},{4,20},{5,53},{6,22},{7,55},{8,24},{9,... | collective-permute-start | bytes 897032 | tf_op jit(solution)/shard_map/ppermute | solution.py:482
  31.2 1.5 %collective-permute-start.3 = (f32[584,128]{1,0:T(8,128)S(1)}, f32[584,128]{1,0:T(8,128)S(1)}, u32[]{:S(2)}, u32[]{:S(2)}) collective-permute-start(f32[584,128]{1,0:T(8,128)S(1)} %get-tuple-element.15), channel_id=1, source_target_pairs={{0,64},{1,67},{2,66},{3,65},{4,68},{5,71},{6,70},{7,69},{8,72},{9,... | collective-permute-start | bytes 897032 | tf_op jit(solution)/shard_map/ppermute | solution.py:482
  32.7 0.0 collective-permute-start.4
  32.7 2.0 %collective-permute-start.5 = (f32[584,128]{1,0:T(8,128)}, f32[584,128]{1,0:T(8,128)S(1)}, u32[]{:S(2)}, u32[]{:S(2)}) collective-permute-start(f32[584,128]{1,0:T(8,128)} %get-tuple-element.17), channel_id=1, source_target_pairs={{0,4},{1,13},{2,6},{3,15},{4,0},{5,9},{6,2},{7,11},{8,12},{9,5},{1... | collective-permute-start | bytes 897032 | tf_op jit(solution)/shard_map/ppermute | solution.py:482
  34.7 1.5 %collective-permute-start.6 = (f32[584,128]{1,0:T(8,128)S(1)}, f32[584,128]{1,0:T(8,128)S(1)}, u32[]{:S(2)}, u32[]{:S(2)}) collective-permute-start(f32[584,128]{1,0:T(8,128)S(1)} %get-tuple-element.18), channel_id=1, source_target_pairs={{0,20},{1,61},{2,22},{3,63},{4,16},{5,57},{6,18},{7,59},{8,28},{9,... | collective-permute-start | bytes 897032 | tf_op jit(solution)/shard_map/ppermute | solution.py:482
  36.2 6.6 %collective-permute-done.2.refs_1_ = f32[584,128]{1,0:T(8,128)S(1)} collective-permute-done((f32[584,128]{1,0:T(8,128)S(1)}, f32[584,128]{1,0:T(8,128)S(1)}, u32[]{:S(2)}, u32[]{:S(2)}) %collective-permute-start.2) | collective-permute-done | bytes 299040 | tf_op jit(solution)/shard_map/ppermute | solution.py:482
  42.7 2.4 %collective-permute-start.7 = (f32[584,128]{1,0:T(8,128)S(1)}, f32[584,128]{1,0:T(8,128)S(1)}, u32[]{:S(2)}, u32[]{:S(2)}) collective-permute-start(f32[584,128]{1,0:T(8,128)S(1)} %get-tuple-element.19), channel_id=1, source_target_pairs={{0,68},{1,79},{2,70},{3,77},{4,64},{5,75},{6,66},{7,73},{8,76},{9,... | collective-permute-start | bytes 897032 | tf_op jit(solution)/shard_map/ppermute | solution.py:482
  45.1 0.0 collective-permute-done.3.refs_2_
  45.1 0.5 collective-permute-start.8
  45.7 0.0 all-to-all-done.even_ref
  45.7 1.8 %add_even.1.even_ref = f32[584,128]{1,0:T(8,128)S(1)} custom-call(f32[8,584,128]{2,1,0:T(8,128)} %all-to-all-done.even_ref), custom_call_target="tpu_custom_call" | custom-call | flops 6000000 | bytes 3000000 | tf_op jit(solution)/shard_map/add_even/pallas_call | solution.py:266
  47.5 0.0 copy-start
  47.5 2.5 %collective-permute-done.4.refs_3_ = f32[584,128]{1,0:T(8,128)S(1)} collective-permute-done((f32[584,128]{1,0:T(8,128)}, f32[584,128]{1,0:T(8,128)S(1)}, u32[]{:S(2)}, u32[]{:S(2)}) %collective-permute-start.4) | collective-permute-done | bytes 299040 | tf_op jit(solution)/shard_map/ppermute | solution.py:482
  50.0 0.0 collective-permute-done.5.refs_4_
  50.0 0.1 collective-permute-done.6.refs_5_
  50.1 2.5 %collective-permute-done.7.refs_6_ = f32[584,128]{1,0:T(8,128)S(1)} collective-permute-done((f32[584,128]{1,0:T(8,128)S(1)}, f32[584,128]{1,0:T(8,128)S(1)}, u32[]{:S(2)}, u32[]{:S(2)}) %collective-permute-start.7) | collective-permute-done | bytes 299040 | tf_op jit(solution)/shard_map/ppermute | solution.py:482
  52.6 3.9 %collective-permute-done.8.refs_7_ = f32[584,128]{1,0:T(8,128)S(1)} collective-permute-done((f32[584,128]{1,0:T(8,128)S(1)}, f32[584,128]{1,0:T(8,128)S(1)}, u32[]{:S(2)}, u32[]{:S(2)}) %collective-permute-start.8) | collective-permute-done | bytes 299040 | tf_op jit(solution)/shard_map/ppermute | solution.py:482
  56.5 1.0 %add_odd.1 = f32[8,152,128]{2,1,0:T(8,128)} custom-call(f32[584,128]{1,0:T(8,128)S(1)} %add_even.1.even_ref, f32[584,128]{1,0:T(8,128)S(1)} %get-tuple-element.13.refs_0_, f32[584,128]{1,0:T(8,128)S(1)} %collective-permute-done.2.refs_1_, f32[584,128]{1,0:T(8,128)S(1)} %collective-permute-done.3.refs_2_, f32[584,128]{1,0:T(8,128)S(1)} %collective-permute-done.4.refs_3_, ...), custom_call_target="tpu_custom_call" | custom-call | tf_op jit(solution)/shard_map/add_odd/pallas_call | solution.py:296
  57.5 9.1 %all-to-all-start.1 = ((f32[8,152,128]{2,1,0:T(8,128)}), f32[8,152,128]{2,1,0:T(8,128)S(1)}, u32[]{:S(2)}, u32[]{:S(2)}) async-start(f32[8,152,128]{2,1,0:T(8,128)} %add_odd.1), calls=%async_computation.1 | async-start | bytes 1245184 | tf_op jit(solution)/shard_map/all_to_all | solution.py:485
  66.6 11.7 %all-to-all-done.1.g_ref = f32[8,152,128]{2,1,0:T(8,128)S(1)} async-done(((f32[8,152,128]{2,1,0:T(8,128)}), f32[8,152,128]{2,1,0:T(8,128)S(1)}, u32[]{:S(2)}, u32[]{:S(2)}) %all-to-all-start.1) | async-done | bytes 622624 | tf_op jit(solution)/shard_map/all_to_all | solution.py:485
  78.3 5.8 %whiten.1 = f32[8,152,128]{2,1,0:T(8,128)S(1)} custom-call(s32[1]{0:T(128)} %bitcast.index_ref, s32[128]{0:T(128)S(1)} %copy-done, f32[8,152,128]{2,1,0:T(8,128)S(1)} %all-to-all-done.1.g_ref), custom_call_target="tpu_custom_call" | custom-call | tf_op jit(solution)/shard_map/whiten/pallas_call | solution.py:422
  84.1 11.6 %all_to_all.15.p_ref = f32[8,152,128]{2,1,0:T(8,128)S(1)} all-to-all(f32[8,152,128]{2,1,0:T(8,128)S(1)} %whiten.1), channel_id=1, replica_groups={{0,16,32,48,64,80,96,112},{1,17,33,49,65,81,97,113},{2,18,34,50,66,82,9..., dimensions={0} | all-to-all | bytes 1245184 | tf_op jit(solution)/shard_map/all_to_all | solution.py:487
  95.7 1.6 %spread.1 = f32[8,192,192]{2,1,0:T(8,128)} custom-call(f32[8,152,128]{2,1,0:T(8,128)S(1)} %all_to_all.15.p_ref), custom_call_target="tpu_custom_call" | custom-call | tf_op jit(solution)/shard_map/spread/pallas_call | solution.py:456
  (1 shorter events, 0.0 us)
Async XLA Ops:
  5.9 5.5 %collective-permute-start = (f32[4640,128]{1,0:T(8,128)}, f32[4640,128]{1,0:T(8,128)}, u32[]{:S(2)}, u32[]{:S(2)}) collective-permute-start(f32[4640,128]{1,0:T(8,128)} %their_grams.2), channel_id=1, source_target_pairs={{0,1},{1,0},{2,3},{3,2},{4,5},{5,4},{6,7},{7,6},{8,9},{9,8},{10,11... | collective-permute-start | bytes 7127048 | tf_op jit(solution)/shard_map/ppermute | solution.py:476
  10.8 12.2 %collective-permute-start.1 = (f32[4640,128]{1,0:T(8,128)S(1)}, f32[4640,128]{1,0:T(8,128)}, u32[]{:S(2)}, u32[]{:S(2)}) collective-permute-start(f32[4640,128]{1,0:T(8,128)S(1)} %their_grams.3), channel_id=1, source_target_pairs={{0,1},{1,0},{2,3},{3,2},{4,5},{5,4},{6,7},{7,6},{8,9},{9,8},{10,11... | collective-permute-start | bytes 7127048 | tf_op jit(solution)/shard_map/ppermute | solution.py:476
  17.7 28.0 %all-to-all-start = ((f32[8,584,128]{2,1,0:T(8,128)}), f32[8,584,128]{2,1,0:T(8,128)}, u32[]{:S(2)}, u32[]{:S(2)}) async-start(f32[8,584,128]{2,1,0:T(8,128)} %my_grams.2), calls=%async_computation | async-start | bytes 4784128 | tf_op jit(solution)/shard_map/all_to_all | solution.py:478
  29.2 13.5 %collective-permute-start.2 = (f32[584,128]{1,0:T(8,128)S(1)}, f32[584,128]{1,0:T(8,128)S(1)}, u32[]{:S(2)}, u32[]{:S(2)}) collective-permute-start(f32[584,128]{1,0:T(8,128)S(1)} %get-tuple-element.14), channel_id=1, source_target_pairs={{0,16},{1,49},{2,18},{3,51},{4,20},{5,53},{6,22},{7,55},{8,24},{9,... | collective-permute-start | bytes 897032 | tf_op jit(solution)/shard_map/ppermute | solution.py:482
  31.2 13.9 %collective-permute-start.3 = (f32[584,128]{1,0:T(8,128)S(1)}, f32[584,128]{1,0:T(8,128)S(1)}, u32[]{:S(2)}, u32[]{:S(2)}) collective-permute-start(f32[584,128]{1,0:T(8,128)S(1)} %get-tuple-element.15), channel_id=1, source_target_pairs={{0,64},{1,67},{2,66},{3,65},{4,68},{5,71},{6,70},{7,69},{8,72},{9,... | collective-permute-start | bytes 897032 | tf_op jit(solution)/shard_map/ppermute | solution.py:482
  32.7 17.3 %collective-permute-start.4 = (f32[584,128]{1,0:T(8,128)}, f32[584,128]{1,0:T(8,128)S(1)}, u32[]{:S(2)}, u32[]{:S(2)}) collective-permute-start(f32[584,128]{1,0:T(8,128)} %get-tuple-element.16), channel_id=1, source_target_pairs={{0,80},{1,115},{2,82},{3,113},{4,84},{5,119},{6,86},{7,117},{8,88}... | collective-permute-start | bytes 897032 | tf_op jit(solution)/shard_map/ppermute | solution.py:482
  32.7 17.3 %collective-permute-start.5 = (f32[584,128]{1,0:T(8,128)}, f32[584,128]{1,0:T(8,128)S(1)}, u32[]{:S(2)}, u32[]{:S(2)}) collective-permute-start(f32[584,128]{1,0:T(8,128)} %get-tuple-element.17), channel_id=1, source_target_pairs={{0,4},{1,13},{2,6},{3,15},{4,0},{5,9},{6,2},{7,11},{8,12},{9,5},{1... | collective-permute-start | bytes 897032 | tf_op jit(solution)/shard_map/ppermute | solution.py:482
  34.7 15.4 %collective-permute-start.6 = (f32[584,128]{1,0:T(8,128)S(1)}, f32[584,128]{1,0:T(8,128)S(1)}, u32[]{:S(2)}, u32[]{:S(2)}) collective-permute-start(f32[584,128]{1,0:T(8,128)S(1)} %get-tuple-element.18), channel_id=1, source_target_pairs={{0,20},{1,61},{2,22},{3,63},{4,16},{5,57},{6,18},{7,59},{8,28},{9,... | collective-permute-start | bytes 897032 | tf_op jit(solution)/shard_map/ppermute | solution.py:482
  42.7 9.8 %collective-permute-start.7 = (f32[584,128]{1,0:T(8,128)S(1)}, f32[584,128]{1,0:T(8,128)S(1)}, u32[]{:S(2)}, u32[]{:S(2)}) collective-permute-start(f32[584,128]{1,0:T(8,128)S(1)} %get-tuple-element.19), channel_id=1, source_target_pairs={{0,68},{1,79},{2,70},{3,77},{4,64},{5,75},{6,66},{7,73},{8,76},{9,... | collective-permute-start | bytes 897032 | tf_op jit(solution)/shard_map/ppermute | solution.py:482
  45.1 11.3 %collective-permute-start.8 = (f32[584,128]{1,0:T(8,128)S(1)}, f32[584,128]{1,0:T(8,128)S(1)}, u32[]{:S(2)}, u32[]{:S(2)}) collective-permute-start(f32[584,128]{1,0:T(8,128)S(1)} %get-tuple-element.20), channel_id=1, source_target_pairs={{0,84},{1,127},{2,86},{3,125},{4,80},{5,123},{6,82},{7,121},{8,92}... | collective-permute-start | bytes 897032 | tf_op jit(solution)/shard_map/ppermute | solution.py:482
  47.5 30.8 %copy-start = (s32[128]{0:T(128)S(1)}, s32[128]{0:T(128)}, u32[]{:S(2)}) copy-start(s32[128]{0:T(128)} %damp_ref.1) | copy-start | bytes 1540
  57.5 20.8 %all-to-all-start.1 = ((f32[8,152,128]{2,1,0:T(8,128)}), f32[8,152,128]{2,1,0:T(8,128)S(1)}, u32[]{:S(2)}, u32[]{:S(2)}) async-start(f32[8,152,128]{2,1,0:T(8,128)} %add_odd.1), calls=%async_computation.1 | async-start | bytes 1245184 | tf_op jit(solution)/shard_map/all_to_all | solution.py:485

commit v2 on v1

--- a/solution.py
+++ b/solution.py
@@ -132,46 +132,47 @@
         w_ref[LANES * i : LANES * (i + 1)] = jnp.broadcast_to(power, (LANES, LANES)).T.astype(jnp.bfloat16)
 
 
-def their_grams_kernel(core_ref, x_ref, exp_ref, o_ref, w_ref):
+def their_grams_kernel(core_ref, xa_ref, xb_ref, exp_ref, o_ref, w_ref):
     i = pl.program_id(0)
 
     @pl.when(i == 0)
     def _():
         spread_weights(exp_ref, w_ref)
 
-    base = BLOCK_ROWS * i if o_ref.shape[0] > BLOCK_ROWS else 0
-
-    def put(index, start, rows):
-        o_ref[pl.ds(pl.multiple_of(base + BODY * index + start, 8), rows.shape[0])] = rows
-
-    def put_diag(index, diag):
-        o_ref[pl.ds(pl.multiple_of(base + 8 * BODY, 8) + index, 1)] = diag
-
-    block_grams(x_ref, w_ref, put, put_diag)
+    for part, x_ref in enumerate((xa_ref, xb_ref)):
+        base = BLOCK_ROWS * (2 * i + part) if o_ref.shape[0] > 2 * BLOCK_ROWS else BLOCK_ROWS * part
+
+        def put(index, start, rows, base=base):
+            o_ref[pl.ds(pl.multiple_of(base + BODY * index + start, 8), rows.shape[0])] = rows
+
+        def put_diag(index, diag, base=base):
+            o_ref[pl.ds(pl.multiple_of(base + 8 * BODY, 8) + index, 1)] = diag
+
+        block_grams(x_ref, w_ref, put, put_diag)
 
 
 def their_grams(projected, weight_exp, core, half):
     tokens = projected.shape[0]
+    x_spec = lambda part: pl.BlockSpec(
+        (tokens, 8 * HD), lambda i, core: (0, 2 * chunk_block(half, 2 * i + part) + 1 - core[0])
+    )
     return pl.pallas_call(
         their_grams_kernel,
         grid_spec=pltpu.PrefetchScalarGridSpec(
             num_scalar_prefetch=1,
-            grid=(4,),
-            in_specs=[
-                pl.BlockSpec((tokens, 8 * HD), lambda i, core: (0, 2 * chunk_block(half, i) + 1 - core[0])),
-                pl.BlockSpec((tokens,), lambda i, core: (0,)),
-            ],
-            out_specs=WHOLE if half else pl.BlockSpec((BLOCK_ROWS, LANES), lambda i, core: (i, 0)),
+            grid=(2,),
+            in_specs=[x_spec(0), x_spec(1), pl.BlockSpec((tokens,), lambda i, core: (0,))],
+            out_specs=pl.BlockSpec((2 * BLOCK_ROWS, LANES), lambda i, core: (i, 0)) if half else WHOLE,
             scratch_shapes=[pltpu.VMEM((tokens, LANES), jnp.bfloat16)],
         ),
-        out_shape=(pltpu.VMEM if half else pltpu.HBM)((4 * BLOCK_ROWS, LANES), jnp.float32),
-        compiler_params=params(12, dimension_semantics=("arbitrary",)),
+        out_shape=(pltpu.HBM if half else pltpu.VMEM)((4 * BLOCK_ROWS, LANES), jnp.float32),
+        compiler_params=params(16, dimension_semantics=("arbitrary",)),
         cost_estimate=pl.CostEstimate(flops=tokens * 64 * HD * HD, bytes_accessed=7_500_000, transcendentals=0),
         name="their_grams",
-    )(core, off_chip(projected), off_chip(weight_exp))
-
-
-def fill_slots(half, core_ref, x_ref, exp_ref, received_ref, all_ref, w_ref):
+    )(core, off_chip(projected), off_chip(projected), off_chip(weight_exp))
+
+
+def fill_slots(half, core_ref, x_refs, exp_ref, received_ref, all_ref, w_ref):
     i = pl.program_id(0)
 
     @pl.when(i == 0)
@@ -180,25 +181,27 @@
         for slot in range(8):
             all_ref[slot, SLOT_ROWS - 8 :] = jnp.zeros((8, LANES), jnp.float32)
 
-    block = chunk_block(half, i)
-    spots = [spot(block, inner, core_ref[0]) for inner in range(8)]
-
-    def put(index, start, rows):
-        slot, rest = spots[index]
-        size = rows.shape[0]
-        at = pl.multiple_of(BODY * rest + start, 8)
-        all_ref[slot, pl.ds(at, size)] = rows + received_ref[BODY * index + start : BODY * index + start + size]
-
-    def put_diag(index, diag):
-        slot, rest = spots[index]
-        all_ref[slot, pl.ds(4 * BODY + rest, 1)] = diag + received_ref[8 * BODY + index : 8 * BODY + index + 1]
-
-    block_grams(x_ref, w_ref, put, put_diag)
-    return spots
-
-
-def my_even_kernel(core_ref, spot_ref, x_ref, exp_ref, received_ref, o_ref, w_ref, all_ref, sem):
-    spots = fill_slots(0, core_ref, x_ref, exp_ref, received_ref, all_ref, w_ref)
+    spots = []
+    for part, x_ref in enumerate(x_refs):
+        spots.append([spot(chunk_block(half, 2 * i + part), inner, core_ref[0]) for inner in range(8)])
+
+        def put(index, start, rows, part=part):
+            slot, rest = spots[part][index]
+            at = pl.ds(pl.multiple_of(BODY * rest + start, 8), rows.shape[0])
+            source = BLOCK_ROWS * part + BODY * index + start
+            all_ref[slot, at] = rows + received_ref[source : source + rows.shape[0]]
+
+        def put_diag(index, diag, part=part):
+            slot, rest = spots[part][index]
+            source = BLOCK_ROWS * part + 8 * BODY + index
+            all_ref[slot, pl.ds(4 * BODY + rest, 1)] = diag + received_ref[source : source + 1]
+
+        block_grams(x_ref, w_ref, put, put_diag)
+    return spots[0] + spots[1]
+
+
+def my_even_kernel(core_ref, spot_ref, xa_ref, xb_ref, exp_ref, received_ref, o_ref, w_ref, all_ref, sem):
+    spots = fill_slots(0, core_ref, (xa_ref, xb_ref), exp_ref, received_ref, all_ref, w_ref)
     for slot, rest in spots:
         rows = pl.ds(pl.multiple_of(BODY * rest, 8), BODY)
         pltpu.make_async_copy(all_ref.at[slot, rows], o_ref.at[slot, rows], sem).start()
@@ -210,9 +213,9 @@
         pltpu.make_async_copy(all_ref, o_ref, sem).wait()
 
 
-def my_odd_kernel(core_ref, spot_ref, x_ref, exp_ref, received_ref, *refs):
+def my_odd_kernel(core_ref, spot_ref, xa_ref, xb_ref, exp_ref, received_ref, *refs):
     outs, (w_ref, all_ref) = refs[:8], refs[8:]
-    fill_slots(1, core_ref, x_ref, exp_ref, received_ref, all_ref, w_ref)
+    fill_slots(1, core_ref, (xa_ref, xb_ref), exp_ref, received_ref, all_ref, w_ref)
 
     @pl.when(pl.program_id(0) == pl.num_programs(0) - 1)
     def _():
@@ -230,24 +233,28 @@
         kernel, outs = my_even_kernel, pl.BlockSpec(memory_space=pl.ANY)
         shapes = pltpu.HBM((8, SLOT_ROWS, LANES), jnp.float32)
         scratch.append(pltpu.SemaphoreType.DMA(()))
+    x_spec = lambda part: pl.BlockSpec(
+        (tokens, 8 * HD), lambda i, core, spot: (0, 2 * chunk_block(half, 2 * i + part) + core[0])
+    )
     return pl.pallas_call(
         kernel,
         grid_spec=pltpu.PrefetchScalarGridSpec(
             num_scalar_prefetch=2,
-            grid=(4,),
+            grid=(2,),
             in_specs=[
-                pl.BlockSpec((tokens, 8 * HD), lambda i, core, spot: (0, 2 * chunk_block(half, i) + core[0])),
+                x_spec(0),
+                x_spec(1),
                 pl.BlockSpec((tokens,), lambda i, core, spot: (0,)),
-                pl.BlockSpec((BLOCK_ROWS, LANES), lambda i, core, spot: (i, 0)),
+                pl.BlockSpec((2 * BLOCK_ROWS, LANES), lambda i, core, spot: (i, 0)),
             ],
             out_specs=outs,
             scratch_shapes=scratch,
         ),
         out_shape=shapes,
-        compiler_params=params(16, dimension_semantics=("arbitrary",)),
+        compiler_params=params(20, dimension_semantics=("arbitrary",)),
         cost_estimate=pl.CostEstimate(flops=tokens * 64 * HD * HD, bytes_accessed=10_000_000, transcendentals=0),
         name="my_grams",
-    )(core, own_spot, off_chip(projected), off_chip(weight_exp), off_chip(received))
+    )(core, own_spot, off_chip(projected), off_chip(projected), off_chip(weight_exp), off_chip(received))
 
 
 def even_kernel(even_ref, o_ref):
@@ -433,15 +440,16 @@
     row = lax.broadcasted_iota(jnp.int32, (HALF, LANES), 0)
     lane = lax.broadcasted_iota(jnp.int32, (HALF, LANES), 1)
     row32, lane32 = row[:32], lane[:32]
-    for i in range(8):
-        middle = p_ref[i, 64:128]
-        tail = p_ref[i, 128:144]
-        diag = p_ref[i, 144:145]
+    first_matrix = o_ref.shape[0] * pl.program_id(0)
+    for i in range(o_ref.shape[0]):
+        middle = p_ref[first_matrix + i, 64:128]
+        tail = p_ref[first_matrix + i, 128:144]
+        diag = p_ref[first_matrix + i, 144:145]
         turned = jnp.concatenate([middle, middle], axis=0).T[HALF:]
         first = jnp.where(lane < row, turned, jnp.where(lane == row, diag, 0.0))
         o_ref[i, 0:64, 0:128] = first
         o_ref[i, 64:128, 0:128] = jnp.where(lane - HALF <= row, middle, 0.0)
-        o_ref[i, 128:192, 0:128] = p_ref[i, 0:64]
+        o_ref[i, 128:192, 0:128] = p_ref[first_matrix + i, 0:64]
         o_ref[i, 0:128, 128:192] = jnp.zeros((128, HALF), jnp.float32)
         lower = jnp.concatenate([tail, rolled(tail, HALF)], axis=0)
         corner = jnp.concatenate([lower] * 4, axis=0).T[32:64]
@@ -455,9 +463,9 @@
 def spread(packed):
     return pl.pallas_call(
         spread_kernel,
-        grid=(1,),
+        grid=(2,),
         in_specs=[WHOLE],
-        out_specs=pl.BlockSpec((8, HD, HD), lambda i: (0, 0, 0)),
+        out_specs=pl.BlockSpec((4, HD, HD), lambda i: (i, 0, 0)),
         out_shape=jax.ShapeDtypeStruct((8, HD, HD), jnp.float32),
         compiler_params=params(8),
         name="spread",

time: 97.8 us -> 95.5 us (0.976)
  Pallas kernels: 33.5 us -> 30.9 us
  waiting for transfers between devices: 27.2 us -> 28.3 us
    pallas_call x2, Pallas kernels: 10.8 us -> 9.5 us  [their_grams(): pl.pallas_call(their_grams_kernel, grid_spec=pltpu.PrefetchScalarGridSpec...]
    pallas_call x2, Pallas kernels: 12.6 us -> 11.4 us  [my_grams(): pl.pallas_call(kernel, grid_spec=pltpu.PrefetchScalarGridSpec(num_scalar_...]
    ppermute x7, waiting for transfers between devices: 15.5 us -> 16.6 us  [on_device(): swapped.append(lax.ppermute(odd[flip], DEVICES, peers(flip)))]
  transfers between devices with their start and end apart: 11 -> 11, of which waited for: 6 -> 6; matrix products, arithmetic and copies ran while one was open for 0% -> 0% of each run, Pallas kernels for 20% -> 19%
where the time goes in v2:
time: 95.5 us; the launch traced here: 95.2 us
  Pallas kernels  30.9 us (32%)
  waiting for transfers between devices  28.3 us (30%)
  starting transfers between devices  24.2 us (25%)
  blocking collectives  11.6 us (12%)
    ppermute x7, waiting for transfers between devices, on_device(): swapped.append(lax.ppermute(odd[flip], DEVICES, peers(flip)))  16.6 us
    all_to_all x1, waiting for transfers between devices, on_device(): lax.all_to_all(cube, DEVICES, 0, 0, tiled=True, axis_index_groups=cubes(1))  11.7 us
    all_to_all x1, blocking collectives, on_device(): lax.all_to_all(factors, DEVICES, 0, 0, tiled=True, axis_index_groups=owne...  11.6 us
    pallas_call x2, Pallas kernels, my_grams(): pl.pallas_call(kernel, grid_spec=pltpu.PrefetchScalarGridSpec(num_scalar_...  11.4 us
    pallas_call x2, Pallas kernels, their_grams(): pl.pallas_call(their_grams_kernel, grid_spec=pltpu.PrefetchScalarGridSpec...  9.5 us
    ppermute x7, starting transfers between devices, on_device(): swapped.append(lax.ppermute(odd[flip], DEVICES, peers(flip)))  9.35 us
    all_to_all x1, starting transfers between devices, on_device(): lax.all_to_all(cube, DEVICES, 0, 0, tiled=True, axis_index_groups=cubes(1))  9.1 us
    pallas_call x1, Pallas kernels, whiten(): pl.pallas_call(whiten_kernel, in_specs=[smem, smem, WHOLE], out_specs=WHO...  5.78 us
  transfers between devices with their start and end apart: 11, of which 6 were waited for; matrix products, arithmetic and copies ran while one was open for 0% of the time, Pallas kernels for 19%

profile of v2, /device:TPU:0, one launch (start us, length us, event | category | flops | bytes accessed | tf_op | source)
XLA Modules:
  0.0 95.2 jit_solution(10309466566950331308)
XLA Ops:
  0.0 4.2 %their_grams.2 = f32[4640,128]{1,0:T(8,128)S(1)} custom-call(s32[1]{0:T(128)} %bitcast.1.core_ref, bf16[384,24576]{1,0:T(8,128)(2,1)} %xb_ref.7, bf16[384,24576]{1,0:T(8,128)(2,1)} %xb_ref.7, s32[384]{0:T(512)} %exp_ref.7), custom_call_target="tpu_custom_call" | custom-call | flops 905969664 | bytes 7500000 | tf_op jit(solution)/shard_map/their_grams/pallas_call | solution.py:159
  4.2 0.1 collective-permute-start
  4.3 5.3 %their_grams.3 = f32[4640,128]{1,0:T(8,128)} custom-call(s32[1]{0:T(128)} %bitcast.1.core_ref, bf16[384,24576]{1,0:T(8,128)(2,1)} %xb_ref.7, bf16[384,24576]{1,0:T(8,128)(2,1)} %xb_ref.7, s32[384]{0:T(512)} %exp_ref.7), custom_call_target="tpu_custom_call" | custom-call | flops 905969664 | bytes 7500000 | tf_op jit(solution)/shard_map/their_grams/pallas_call | solution.py:159
  9.6 0.5 collective-permute-start.1
  10.1 0.0 collective-permute-done.received_ref
  10.1 5.7 %my_grams.2 = f32[8,584,128]{2,1,0:T(8,128)} custom-call(s32[1]{0:T(128)} %bitcast.1.core_ref, s32[1]{0:T(128)} %bitcast.2.spot_ref, bf16[384,24576]{1,0:T(8,128)(2,1)} %xb_ref.7, bf16[384,24576]{1,0:T(8,128)(2,1)} %xb_ref.7, s32[384]{0:T(512)} %exp_ref.7, f32[4640,128]{1,0:T(8,128)} %collective-permute-done.received_ref), custom_call_target="tpu_custom_call" | custom-call | flops 905969664 | bytes 10000000 | tf_op jit(solution)/shard_map/my_grams/pallas_call | solution.py:239
  15.8 5.2 %all-to-all-start = ((f32[8,584,128]{2,1,0:T(8,128)}), f32[8,584,128]{2,1,0:T(8,128)}, u32[]{:S(2)}, u32[]{:S(2)}) async-start(f32[8,584,128]{2,1,0:T(8,128)} %my_grams.2), calls=%async_computation | async-start | bytes 4784128 | tf_op jit(solution)/shard_map/all_to_all | solution.py:486
  21.0 0.0 collective-permute-done.1.received_ref
  21.0 5.6 %my_grams.3 = (f32[584,128]{1,0:T(8,128)S(1)}, f32[584,128]{1,0:T(8,128)S(1)}, f32[584,128]{1,0:T(8,128)S(1)}, f32[584,128]{1,0:T(8,128)}, f32[584,128]{1,0:T(8,...) custom-call(s32[1]{0:T(128)} %bitcast.1.core_ref, s32[1]{0:T(128)} %bitcast.2.spot_ref, ...), custom_call_target="tpu_custom_call" | custom-call | flops 905969664 | bytes 10000000 | tf_op jit(solution)/shard_map/my_grams/pallas_call | solution.py:239
  26.7 2.0 %collective-permute-start.2 = (f32[584,128]{1,0:T(8,128)S(1)}, f32[584,128]{1,0:T(8,128)S(1)}, u32[]{:S(2)}, u32[]{:S(2)}) collective-permute-start(f32[584,128]{1,0:T(8,128)S(1)} %get-tuple-element.14), channel_id=1, source_target_pairs={{0,16},{1,49},{2,18},{3,51},{4,20},{5,53},{6,22},{7,55},{8,24},{9,... | collective-permute-start | bytes 897032 | tf_op jit(solution)/shard_map/ppermute | solution.py:490
  28.7 1.5 %collective-permute-start.3 = (f32[584,128]{1,0:T(8,128)S(1)}, f32[584,128]{1,0:T(8,128)S(1)}, u32[]{:S(2)}, u32[]{:S(2)}) collective-permute-start(f32[584,128]{1,0:T(8,128)S(1)} %get-tuple-element.15), channel_id=1, source_target_pairs={{0,64},{1,67},{2,66},{3,65},{4,68},{5,71},{6,70},{7,69},{8,72},{9,... | collective-permute-start | bytes 897032 | tf_op jit(solution)/shard_map/ppermute | solution.py:490
  30.1 0.0 collective-permute-start.4
  30.2 2.0 %collective-permute-start.5 = (f32[584,128]{1,0:T(8,128)}, f32[584,128]{1,0:T(8,128)S(1)}, u32[]{:S(2)}, u32[]{:S(2)}) collective-permute-start(f32[584,128]{1,0:T(8,128)} %get-tuple-element.17), channel_id=1, source_target_pairs={{0,4},{1,13},{2,6},{3,15},{4,0},{5,9},{6,2},{7,11},{8,12},{9,5},{1... | collective-permute-start | bytes 897032 | tf_op jit(solution)/shard_map/ppermute | solution.py:490
  32.2 1.5 %collective-permute-start.6 = (f32[584,128]{1,0:T(8,128)S(1)}, f32[584,128]{1,0:T(8,128)S(1)}, u32[]{:S(2)}, u32[]{:S(2)}) collective-permute-start(f32[584,128]{1,0:T(8,128)S(1)} %get-tuple-element.18), channel_id=1, source_target_pairs={{0,20},{1,61},{2,22},{3,63},{4,16},{5,57},{6,18},{7,59},{8,28},{9,... | collective-permute-start | bytes 897032 | tf_op jit(solution)/shard_map/ppermute | solution.py:490
  33.6 7.2 %collective-permute-done.2.refs_1_ = f32[584,128]{1,0:T(8,128)S(1)} collective-permute-done((f32[584,128]{1,0:T(8,128)S(1)}, f32[584,128]{1,0:T(8,128)S(1)}, u32[]{:S(2)}, u32[]{:S(2)}) %collective-permute-start.2) | collective-permute-done | bytes 299040 | tf_op jit(solution)/shard_map/ppermute | solution.py:490
  40.8 2.4 %collective-permute-start.7 = (f32[584,128]{1,0:T(8,128)S(1)}, f32[584,128]{1,0:T(8,128)S(1)}, u32[]{:S(2)}, u32[]{:S(2)}) collective-permute-start(f32[584,128]{1,0:T(8,128)S(1)} %get-tuple-element.19), channel_id=1, source_target_pairs={{0,68},{1,79},{2,70},{3,77},{4,64},{5,75},{6,66},{7,73},{8,76},{9,... | collective-permute-start | bytes 897032 | tf_op jit(solution)/shard_map/ppermute | solution.py:490
  43.2 0.0 collective-permute-done.3.refs_2_
  43.2 0.0 collective-permute-start.8
  43.2 0.0 all-to-all-done.even_ref
  43.2 1.8 %add_even.1.even_ref = f32[584,128]{1,0:T(8,128)S(1)} custom-call(f32[8,584,128]{2,1,0:T(8,128)} %all-to-all-done.even_ref), custom_call_target="tpu_custom_call" | custom-call | flops 6000000 | bytes 3000000 | tf_op jit(solution)/shard_map/add_even/pallas_call | solution.py:273
  45.1 0.0 copy-start
  45.1 3.0 %collective-permute-done.4.refs_3_ = f32[584,128]{1,0:T(8,128)S(1)} collective-permute-done((f32[584,128]{1,0:T(8,128)}, f32[584,128]{1,0:T(8,128)S(1)}, u32[]{:S(2)}, u32[]{:S(2)}) %collective-permute-start.4) | collective-permute-done | bytes 299040 | tf_op jit(solution)/shard_map/ppermute | solution.py:490
  48.1 0.0 collective-permute-done.5.refs_4_
  48.1 0.1 collective-permute-done.6.refs_5_
  48.2 2.4 %collective-permute-done.7.refs_6_ = f32[584,128]{1,0:T(8,128)S(1)} collective-permute-done((f32[584,128]{1,0:T(8,128)S(1)}, f32[584,128]{1,0:T(8,128)S(1)}, u32[]{:S(2)}, u32[]{:S(2)}) %collective-permute-start.7) | collective-permute-done | bytes 299040 | tf_op jit(solution)/shard_map/ppermute | solution.py:490
  50.6 3.9 %collective-permute-done.8.refs_7_ = f32[584,128]{1,0:T(8,128)S(1)} collective-permute-done((f32[584,128]{1,0:T(8,128)S(1)}, f32[584,128]{1,0:T(8,128)S(1)}, u32[]{:S(2)}, u32[]{:S(2)}) %collective-permute-start.8) | collective-permute-done | bytes 299040 | tf_op jit(solution)/shard_map/ppermute | solution.py:490
  54.5 1.0 %add_odd.1 = f32[8,152,128]{2,1,0:T(8,128)} custom-call(f32[584,128]{1,0:T(8,128)S(1)} %add_even.1.even_ref, f32[584,128]{1,0:T(8,128)S(1)} %get-tuple-element.13.refs_0_, f32[584,128]{1,0:T(8,128)S(1)} %collective-permute-done.2.refs_1_, f32[584,128]{1,0:T(8,128)S(1)} %collective-permute-done.3.refs_2_, f32[584,128]{1,0:T(8,128)S(1)} %collective-permute-done.4.refs_3_, ...), custom_call_target="tpu_custom_call" | custom-call | tf_op jit(solution)/shard_map/add_odd/pallas_call | solution.py:303
  55.5 9.1 %all-to-all-start.1 = ((f32[8,152,128]{2,1,0:T(8,128)}), f32[8,152,128]{2,1,0:T(8,128)S(1)}, u32[]{:S(2)}, u32[]{:S(2)}) async-start(f32[8,152,128]{2,1,0:T(8,128)} %add_odd.1), calls=%async_computation.1 | async-start | bytes 1245184 | tf_op jit(solution)/shard_map/all_to_all | solution.py:493
  64.6 11.7 %all-to-all-done.1.g_ref = f32[8,152,128]{2,1,0:T(8,128)S(1)} async-done(((f32[8,152,128]{2,1,0:T(8,128)}), f32[8,152,128]{2,1,0:T(8,128)S(1)}, u32[]{:S(2)}, u32[]{:S(2)}) %all-to-all-start.1) | async-done | bytes 622624 | tf_op jit(solution)/shard_map/all_to_all | solution.py:493
  76.3 5.8 %whiten.1 = f32[8,152,128]{2,1,0:T(8,128)S(1)} custom-call(s32[1]{0:T(128)} %bitcast.index_ref, s32[128]{0:T(128)S(1)} %copy-done, f32[8,152,128]{2,1,0:T(8,128)S(1)} %all-to-all-done.1.g_ref), custom_call_target="tpu_custom_call" | custom-call | tf_op jit(solution)/shard_map/whiten/pallas_call | solution.py:429
  82.1 11.6 %all_to_all.15.p_ref = f32[8,152,128]{2,1,0:T(8,128)S(1)} all-to-all(f32[8,152,128]{2,1,0:T(8,128)S(1)} %whiten.1), channel_id=1, replica_groups={{0,16,32,48,64,80,96,112},{1,17,33,49,65,81,97,113},{2,18,34,50,66,82,9..., dimensions={0} | all-to-all | bytes 1245184 | tf_op jit(solution)/shard_map/all_to_all | solution.py:495
  93.8 1.4 %spread.1 = f32[8,192,192]{2,1,0:T(8,128)} custom-call(f32[8,152,128]{2,1,0:T(8,128)S(1)} %all_to_all.15.p_ref), custom_call_target="tpu_custom_call" | custom-call | tf_op jit(solution)/shard_map/spread/pallas_call | solution.py:464
  (1 shorter events, 0.0 us)
Async XLA Ops:
  4.2 5.9 %collective-permute-start = (f32[4640,128]{1,0:T(8,128)S(1)}, f32[4640,128]{1,0:T(8,128)}, u32[]{:S(2)}, u32[]{:S(2)}) collective-permute-start(f32[4640,128]{1,0:T(8,128)S(1)} %their_grams.2), channel_id=1, source_target_pairs={{0,1},{1,0},{2,3},{3,2},{4,5},{5,4},{6,7},{7,6},{8,9},{9,8},{10,11... | collective-permute-start | bytes 7127048 | tf_op jit(solution)/shard_map/ppermute | solution.py:484
  9.6 11.4 %collective-permute-start.1 = (f32[4640,128]{1,0:T(8,128)}, f32[4640,128]{1,0:T(8,128)}, u32[]{:S(2)}, u32[]{:S(2)}) collective-permute-start(f32[4640,128]{1,0:T(8,128)} %their_grams.3), channel_id=1, source_target_pairs={{0,1},{1,0},{2,3},{3,2},{4,5},{5,4},{6,7},{7,6},{8,9},{9,8},{10,11... | collective-permute-start | bytes 7127048 | tf_op jit(solution)/shard_map/ppermute | solution.py:484
  15.8 27.4 %all-to-all-start = ((f32[8,584,128]{2,1,0:T(8,128)}), f32[8,584,128]{2,1,0:T(8,128)}, u32[]{:S(2)}, u32[]{:S(2)}) async-start(f32[8,584,128]{2,1,0:T(8,128)} %my_grams.2), calls=%async_computation | async-start | bytes 4784128 | tf_op jit(solution)/shard_map/all_to_all | solution.py:486
  26.7 14.1 %collective-permute-start.2 = (f32[584,128]{1,0:T(8,128)S(1)}, f32[584,128]{1,0:T(8,128)S(1)}, u32[]{:S(2)}, u32[]{:S(2)}) collective-permute-start(f32[584,128]{1,0:T(8,128)S(1)} %get-tuple-element.14), channel_id=1, source_target_pairs={{0,16},{1,49},{2,18},{3,51},{4,20},{5,53},{6,22},{7,55},{8,24},{9,... | collective-permute-start | bytes 897032 | tf_op jit(solution)/shard_map/ppermute | solution.py:490
  28.7 14.5 %collective-permute-start.3 = (f32[584,128]{1,0:T(8,128)S(1)}, f32[584,128]{1,0:T(8,128)S(1)}, u32[]{:S(2)}, u32[]{:S(2)}) collective-permute-start(f32[584,128]{1,0:T(8,128)S(1)} %get-tuple-element.15), channel_id=1, source_target_pairs={{0,64},{1,67},{2,66},{3,65},{4,68},{5,71},{6,70},{7,69},{8,72},{9,... | collective-permute-start | bytes 897032 | tf_op jit(solution)/shard_map/ppermute | solution.py:490
  30.1 17.9 %collective-permute-start.4 = (f32[584,128]{1,0:T(8,128)}, f32[584,128]{1,0:T(8,128)S(1)}, u32[]{:S(2)}, u32[]{:S(2)}) collective-permute-start(f32[584,128]{1,0:T(8,128)} %get-tuple-element.16), channel_id=1, source_target_pairs={{0,80},{1,115},{2,82},{3,113},{4,84},{5,119},{6,86},{7,117},{8,88}... | collective-permute-start | bytes 897032 | tf_op jit(solution)/shard_map/ppermute | solution.py:490
  30.2 17.9 %collective-permute-start.5 = (f32[584,128]{1,0:T(8,128)}, f32[584,128]{1,0:T(8,128)S(1)}, u32[]{:S(2)}, u32[]{:S(2)}) collective-permute-start(f32[584,128]{1,0:T(8,128)} %get-tuple-element.17), channel_id=1, source_target_pairs={{0,4},{1,13},{2,6},{3,15},{4,0},{5,9},{6,2},{7,11},{8,12},{9,5},{1... | collective-permute-start | bytes 897032 | tf_op jit(solution)/shard_map/ppermute | solution.py:490
  32.2 16.0 %collective-permute-start.6 = (f32[584,128]{1,0:T(8,128)S(1)}, f32[584,128]{1,0:T(8,128)S(1)}, u32[]{:S(2)}, u32[]{:S(2)}) collective-permute-start(f32[584,128]{1,0:T(8,128)S(1)} %get-tuple-element.18), channel_id=1, source_target_pairs={{0,20},{1,61},{2,22},{3,63},{4,16},{5,57},{6,18},{7,59},{8,28},{9,... | collective-permute-start | bytes 897032 | tf_op jit(solution)/shard_map/ppermute | solution.py:490
  40.8 9.8 %collective-permute-start.7 = (f32[584,128]{1,0:T(8,128)S(1)}, f32[584,128]{1,0:T(8,128)S(1)}, u32[]{:S(2)}, u32[]{:S(2)}) collective-permute-start(f32[584,128]{1,0:T(8,128)S(1)} %get-tuple-element.19), channel_id=1, source_target_pairs={{0,68},{1,79},{2,70},{3,77},{4,64},{5,75},{6,66},{7,73},{8,76},{9,... | collective-permute-start | bytes 897032 | tf_op jit(solution)/shard_map/ppermute | solution.py:490
  43.2 11.3 %collective-permute-start.8 = (f32[584,128]{1,0:T(8,128)S(1)}, f32[584,128]{1,0:T(8,128)S(1)}, u32[]{:S(2)}, u32[]{:S(2)}) collective-permute-start(f32[584,128]{1,0:T(8,128)S(1)} %get-tuple-element.20), channel_id=1, source_target_pairs={{0,84},{1,127},{2,86},{3,125},{4,80},{5,123},{6,82},{7,121},{8,92}... | collective-permute-start | bytes 897032 | tf_op jit(solution)/shard_map/ppermute | solution.py:490
  45.1 31.3 %copy-start = (s32[128]{0:T(128)S(1)}, s32[128]{0:T(128)}, u32[]{:S(2)}) copy-start(s32[128]{0:T(128)} %damp_ref.1) | copy-start | bytes 1540
  55.5 20.8 %all-to-all-start.1 = ((f32[8,152,128]{2,1,0:T(8,128)}), f32[8,152,128]{2,1,0:T(8,128)S(1)}, u32[]{:S(2)}, u32[]{:S(2)}) async-start(f32[8,152,128]{2,1,0:T(8,128)} %add_odd.1), calls=%async_computation.1 | async-start | bytes 1245184 | tf_op jit(solution)/shard_map/all_to_all | solution.py:493

commit v3 on v2

--- a/solution.py
+++ b/solution.py
@@ -172,7 +172,7 @@
     )(core, off_chip(projected), off_chip(projected), off_chip(weight_exp))
 
 
-def fill_slots(half, core_ref, x_refs, exp_ref, received_ref, all_ref, w_ref):
+def fill_slots(half, core_ref, x_refs, exp_ref, received_ref, all_ref, w_ref, packed=lambda spots: None):
     i = pl.program_id(0)
 
     @pl.when(i == 0)
@@ -197,14 +197,16 @@
             all_ref[slot, pl.ds(4 * BODY + rest, 1)] = diag + received_ref[source : source + 1]
 
         block_grams(x_ref, w_ref, put, put_diag)
-    return spots[0] + spots[1]
+        packed(spots[part])
 
 
 def my_even_kernel(core_ref, spot_ref, xa_ref, xb_ref, exp_ref, received_ref, o_ref, w_ref, all_ref, sem):
-    spots = fill_slots(0, core_ref, (xa_ref, xb_ref), exp_ref, received_ref, all_ref, w_ref)
-    for slot, rest in spots:
-        rows = pl.ds(pl.multiple_of(BODY * rest, 8), BODY)
-        pltpu.make_async_copy(all_ref.at[slot, rows], o_ref.at[slot, rows], sem).start()
+    def packed(spots):
+        for slot, rest in spots:
+            rows = pl.ds(pl.multiple_of(BODY * rest, 8), BODY)
+            pltpu.make_async_copy(all_ref.at[slot, rows], o_ref.at[slot, rows], sem).start()
+
+    fill_slots(0, core_ref, (xa_ref, xb_ref), exp_ref, received_ref, all_ref, w_ref, packed)
 
     @pl.when(pl.program_id(0) == pl.num_programs(0) - 1)
     def _():

time: 95.5 us -> 95.3 us (level)
  no operation moved by 1% of the time
where the time goes in v3:
time: 95.3 us; the launch traced here: 95 us
  Pallas kernels  30.7 us (32%)
  waiting for transfers between devices  28.3 us (30%)
  starting transfers between devices  24.3 us (25%)
  blocking collectives  11.6 us (12%)
    ppermute x7, waiting for transfers between devices, on_device(): swapped.append(lax.ppermute(odd[flip], DEVICES, peers(flip)))  16.6 us
    all_to_all x1, waiting for transfers between devices, on_device(): lax.all_to_all(cube, DEVICES, 0, 0, tiled=True, axis_index_groups=cubes(1))  11.7 us
    all_to_all x1, blocking collectives, on_device(): lax.all_to_all(factors, DEVICES, 0, 0, tiled=True, axis_index_groups=owne...  11.6 us
    pallas_call x2, Pallas kernels, my_grams(): pl.pallas_call(kernel, grid_spec=pltpu.PrefetchScalarGridSpec(num_scalar_...  11.1 us
    pallas_call x2, Pallas kernels, their_grams(): pl.pallas_call(their_grams_kernel, grid_spec=pltpu.PrefetchScalarGridSpec...  9.5 us
    ppermute x7, starting transfers between devices, on_device(): swapped.append(lax.ppermute(odd[flip], DEVICES, peers(flip)))  9.36 us
    all_to_all x1, starting transfers between devices, on_device(): lax.all_to_all(cube, DEVICES, 0, 0, tiled=True, axis_index_groups=cubes(1))  9.11 us
    pallas_call x1, Pallas kernels, whiten(): pl.pallas_call(whiten_kernel, in_specs=[smem, smem, WHOLE], out_specs=WHO...  5.78 us
  transfers between devices with their start and end apart: 11, of which 6 were waited for; matrix products, arithmetic and copies ran while one was open for 0% of the time, Pallas kernels for 19%

profile of v3, /device:TPU:0, one launch (start us, length us, event | category | flops | bytes accessed | tf_op | source)
XLA Modules:
  0.0 95.0 jit_solution(10801179054366772115)
XLA Ops:
  0.0 4.2 %their_grams.2 = f32[4640,128]{1,0:T(8,128)S(1)} custom-call(s32[1]{0:T(128)} %bitcast.1.core_ref, bf16[384,24576]{1,0:T(8,128)(2,1)} %xb_ref.7, bf16[384,24576]{1,0:T(8,128)(2,1)} %xb_ref.7, s32[384]{0:T(512)} %exp_ref.7), custom_call_target="tpu_custom_call" | custom-call | flops 905969664 | bytes 7500000 | tf_op jit(solution)/shard_map/their_grams/pallas_call | solution.py:159
  4.2 0.1 collective-permute-start
  4.3 5.3 %their_grams.3 = f32[4640,128]{1,0:T(8,128)} custom-call(s32[1]{0:T(128)} %bitcast.1.core_ref, bf16[384,24576]{1,0:T(8,128)(2,1)} %xb_ref.7, bf16[384,24576]{1,0:T(8,128)(2,1)} %xb_ref.7, s32[384]{0:T(512)} %exp_ref.7), custom_call_target="tpu_custom_call" | custom-call | flops 905969664 | bytes 7500000 | tf_op jit(solution)/shard_map/their_grams/pallas_call | solution.py:159
  9.6 0.5 collective-permute-start.1
  10.1 0.0 collective-permute-done.received_ref
  10.1 5.5 %my_grams.2 = f32[8,584,128]{2,1,0:T(8,128)} custom-call(s32[1]{0:T(128)} %bitcast.1.core_ref, s32[1]{0:T(128)} %bitcast.2.spot_ref, bf16[384,24576]{1,0:T(8,128)(2,1)} %xb_ref.7, bf16[384,24576]{1,0:T(8,128)(2,1)} %xb_ref.7, s32[384]{0:T(512)} %exp_ref.7, f32[4640,128]{1,0:T(8,128)} %collective-permute-done.received_ref), custom_call_target="tpu_custom_call" | custom-call | flops 905969664 | bytes 10000000 | tf_op jit(solution)/shard_map/my_grams/pallas_call | solution.py:241
  15.6 5.2 %all-to-all-start = ((f32[8,584,128]{2,1,0:T(8,128)}), f32[8,584,128]{2,1,0:T(8,128)}, u32[]{:S(2)}, u32[]{:S(2)}) async-start(f32[8,584,128]{2,1,0:T(8,128)} %my_grams.2), calls=%async_computation | async-start | bytes 4784128 | tf_op jit(solution)/shard_map/all_to_all | solution.py:488
  20.8 0.0 collective-permute-done.1.received_ref
  20.8 5.6 %my_grams.3 = (f32[584,128]{1,0:T(8,128)S(1)}, f32[584,128]{1,0:T(8,128)S(1)}, f32[584,128]{1,0:T(8,128)S(1)}, f32[584,128]{1,0:T(8,128)}, f32[584,128]{1,0:T(8,...) custom-call(s32[1]{0:T(128)} %bitcast.1.core_ref, s32[1]{0:T(128)} %bitcast.2.spot_ref, ...), custom_call_target="tpu_custom_call" | custom-call | flops 905969664 | bytes 10000000 | tf_op jit(solution)/shard_map/my_grams/pallas_call | solution.py:241
  26.5 2.0 %collective-permute-start.2 = (f32[584,128]{1,0:T(8,128)S(1)}, f32[584,128]{1,0:T(8,128)S(1)}, u32[]{:S(2)}, u32[]{:S(2)}) collective-permute-start(f32[584,128]{1,0:T(8,128)S(1)} %get-tuple-element.14), channel_id=1, source_target_pairs={{0,16},{1,49},{2,18},{3,51},{4,20},{5,53},{6,22},{7,55},{8,24},{9,... | collective-permute-start | bytes 897032 | tf_op jit(solution)/shard_map/ppermute | solution.py:492
  28.5 1.5 %collective-permute-start.3 = (f32[584,128]{1,0:T(8,128)S(1)}, f32[584,128]{1,0:T(8,128)S(1)}, u32[]{:S(2)}, u32[]{:S(2)}) collective-permute-start(f32[584,128]{1,0:T(8,128)S(1)} %get-tuple-element.15), channel_id=1, source_target_pairs={{0,64},{1,67},{2,66},{3,65},{4,68},{5,71},{6,70},{7,69},{8,72},{9,... | collective-permute-start | bytes 897032 | tf_op jit(solution)/shard_map/ppermute | solution.py:492
  29.9 0.0 collective-permute-start.4
  29.9 2.0 %collective-permute-start.5 = (f32[584,128]{1,0:T(8,128)}, f32[584,128]{1,0:T(8,128)S(1)}, u32[]{:S(2)}, u32[]{:S(2)}) collective-permute-start(f32[584,128]{1,0:T(8,128)} %get-tuple-element.17), channel_id=1, source_target_pairs={{0,4},{1,13},{2,6},{3,15},{4,0},{5,9},{6,2},{7,11},{8,12},{9,5},{1... | collective-permute-start | bytes 897032 | tf_op jit(solution)/shard_map/ppermute | solution.py:492
  31.9 1.5 %collective-permute-start.6 = (f32[584,128]{1,0:T(8,128)S(1)}, f32[584,128]{1,0:T(8,128)S(1)}, u32[]{:S(2)}, u32[]{:S(2)}) collective-permute-start(f32[584,128]{1,0:T(8,128)S(1)} %get-tuple-element.18), channel_id=1, source_target_pairs={{0,20},{1,61},{2,22},{3,63},{4,16},{5,57},{6,18},{7,59},{8,28},{9,... | collective-permute-start | bytes 897032 | tf_op jit(solution)/shard_map/ppermute | solution.py:492
  33.4 7.2 %collective-permute-done.2.refs_1_ = f32[584,128]{1,0:T(8,128)S(1)} collective-permute-done((f32[584,128]{1,0:T(8,128)S(1)}, f32[584,128]{1,0:T(8,128)S(1)}, u32[]{:S(2)}, u32[]{:S(2)}) %collective-permute-start.2) | collective-permute-done | bytes 299040 | tf_op jit(solution)/shard_map/ppermute | solution.py:492
  40.6 2.4 %collective-permute-start.7 = (f32[584,128]{1,0:T(8,128)S(1)}, f32[584,128]{1,0:T(8,128)S(1)}, u32[]{:S(2)}, u32[]{:S(2)}) collective-permute-start(f32[584,128]{1,0:T(8,128)S(1)} %get-tuple-element.19), channel_id=1, source_target_pairs={{0,68},{1,79},{2,70},{3,77},{4,64},{5,75},{6,66},{7,73},{8,76},{9,... | collective-permute-start | bytes 897032 | tf_op jit(solution)/shard_map/ppermute | solution.py:492
  43.0 0.0 collective-permute-done.3.refs_2_
  43.0 0.0 collective-permute-start.8
  43.0 0.0 all-to-all-done.even_ref
  43.0 1.8 %add_even.1.even_ref = f32[584,128]{1,0:T(8,128)S(1)} custom-call(f32[8,584,128]{2,1,0:T(8,128)} %all-to-all-done.even_ref), custom_call_target="tpu_custom_call" | custom-call | flops 6000000 | bytes 3000000 | tf_op jit(solution)/shard_map/add_even/pallas_call | solution.py:275
  44.9 0.0 copy-start
  44.9 3.0 %collective-permute-done.4.refs_3_ = f32[584,128]{1,0:T(8,128)S(1)} collective-permute-done((f32[584,128]{1,0:T(8,128)}, f32[584,128]{1,0:T(8,128)S(1)}, u32[]{:S(2)}, u32[]{:S(2)}) %collective-permute-start.4) | collective-permute-done | bytes 299040 | tf_op jit(solution)/shard_map/ppermute | solution.py:492
  47.9 0.0 collective-permute-done.5.refs_4_
  47.9 0.1 collective-permute-done.6.refs_5_
  48.0 2.4 %collective-permute-done.7.refs_6_ = f32[584,128]{1,0:T(8,128)S(1)} collective-permute-done((f32[584,128]{1,0:T(8,128)S(1)}, f32[584,128]{1,0:T(8,128)S(1)}, u32[]{:S(2)}, u32[]{:S(2)}) %collective-permute-start.7) | collective-permute-done | bytes 299040 | tf_op jit(solution)/shard_map/ppermute | solution.py:492
  50.4 3.9 %collective-permute-done.8.refs_7_ = f32[584,128]{1,0:T(8,128)S(1)} collective-permute-done((f32[584,128]{1,0:T(8,128)S(1)}, f32[584,128]{1,0:T(8,128)S(1)}, u32[]{:S(2)}, u32[]{:S(2)}) %collective-permute-start.8) | collective-permute-done | bytes 299040 | tf_op jit(solution)/shard_map/ppermute | solution.py:492
  54.3 1.0 %add_odd.1 = f32[8,152,128]{2,1,0:T(8,128)} custom-call(f32[584,128]{1,0:T(8,128)S(1)} %add_even.1.even_ref, f32[584,128]{1,0:T(8,128)S(1)} %get-tuple-element.13.refs_0_, f32[584,128]{1,0:T(8,128)S(1)} %collective-permute-done.2.refs_1_, f32[584,128]{1,0:T(8,128)S(1)} %collective-permute-done.3.refs_2_, f32[584,128]{1,0:T(8,128)S(1)} %collective-permute-done.4.refs_3_, ...), custom_call_target="tpu_custom_call" | custom-call | tf_op jit(solution)/shard_map/add_odd/pallas_call | solution.py:305
  55.3 9.1 %all-to-all-start.1 = ((f32[8,152,128]{2,1,0:T(8,128)}), f32[8,152,128]{2,1,0:T(8,128)S(1)}, u32[]{:S(2)}, u32[]{:S(2)}) async-start(f32[8,152,128]{2,1,0:T(8,128)} %add_odd.1), calls=%async_computation.1 | async-start | bytes 1245184 | tf_op jit(solution)/shard_map/all_to_all | solution.py:495
  64.4 11.7 %all-to-all-done.1.g_ref = f32[8,152,128]{2,1,0:T(8,128)S(1)} async-done(((f32[8,152,128]{2,1,0:T(8,128)}), f32[8,152,128]{2,1,0:T(8,128)S(1)}, u32[]{:S(2)}, u32[]{:S(2)}) %all-to-all-start.1) | async-done | bytes 622624 | tf_op jit(solution)/shard_map/all_to_all | solution.py:495
  76.1 5.8 %whiten.1 = f32[8,152,128]{2,1,0:T(8,128)S(1)} custom-call(s32[1]{0:T(128)} %bitcast.index_ref, s32[128]{0:T(128)S(1)} %copy-done, f32[8,152,128]{2,1,0:T(8,128)S(1)} %all-to-all-done.1.g_ref), custom_call_target="tpu_custom_call" | custom-call | tf_op jit(solution)/shard_map/whiten/pallas_call | solution.py:431
  81.9 11.6 %all_to_all.15.p_ref = f32[8,152,128]{2,1,0:T(8,128)S(1)} all-to-all(f32[8,152,128]{2,1,0:T(8,128)S(1)} %whiten.1), channel_id=1, replica_groups={{0,16,32,48,64,80,96,112},{1,17,33,49,65,81,97,113},{2,18,34,50,66,82,9..., dimensions={0} | all-to-all | bytes 1245184 | tf_op jit(solution)/shard_map/all_to_all | solution.py:497
  93.6 1.4 %spread.1 = f32[8,192,192]{2,1,0:T(8,128)} custom-call(f32[8,152,128]{2,1,0:T(8,128)S(1)} %all_to_all.15.p_ref), custom_call_target="tpu_custom_call" | custom-call | tf_op jit(solution)/shard_map/spread/pallas_call | solution.py:466
  (1 shorter events, 0.0 us)
Async XLA Ops:
  4.2 5.9 %collective-permute-start = (f32[4640,128]{1,0:T(8,128)S(1)}, f32[4640,128]{1,0:T(8,128)}, u32[]{:S(2)}, u32[]{:S(2)}) collective-permute-start(f32[4640,128]{1,0:T(8,128)S(1)} %their_grams.2), channel_id=1, source_target_pairs={{0,1},{1,0},{2,3},{3,2},{4,5},{5,4},{6,7},{7,6},{8,9},{9,8},{10,11... | collective-permute-start | bytes 7127048 | tf_op jit(solution)/shard_map/ppermute | solution.py:486
  9.6 11.2 %collective-permute-start.1 = (f32[4640,128]{1,0:T(8,128)}, f32[4640,128]{1,0:T(8,128)}, u32[]{:S(2)}, u32[]{:S(2)}) collective-permute-start(f32[4640,128]{1,0:T(8,128)} %their_grams.3), channel_id=1, source_target_pairs={{0,1},{1,0},{2,3},{3,2},{4,5},{5,4},{6,7},{7,6},{8,9},{9,8},{10,11... | collective-permute-start | bytes 7127048 | tf_op jit(solution)/shard_map/ppermute | solution.py:486
  15.6 27.4 %all-to-all-start = ((f32[8,584,128]{2,1,0:T(8,128)}), f32[8,584,128]{2,1,0:T(8,128)}, u32[]{:S(2)}, u32[]{:S(2)}) async-start(f32[8,584,128]{2,1,0:T(8,128)} %my_grams.2), calls=%async_computation | async-start | bytes 4784128 | tf_op jit(solution)/shard_map/all_to_all | solution.py:488
  26.5 14.1 %collective-permute-start.2 = (f32[584,128]{1,0:T(8,128)S(1)}, f32[584,128]{1,0:T(8,128)S(1)}, u32[]{:S(2)}, u32[]{:S(2)}) collective-permute-start(f32[584,128]{1,0:T(8,128)S(1)} %get-tuple-element.14), channel_id=1, source_target_pairs={{0,16},{1,49},{2,18},{3,51},{4,20},{5,53},{6,22},{7,55},{8,24},{9,... | collective-permute-start | bytes 897032 | tf_op jit(solution)/shard_map/ppermute | solution.py:492
  28.5 14.5 %collective-permute-start.3 = (f32[584,128]{1,0:T(8,128)S(1)}, f32[584,128]{1,0:T(8,128)S(1)}, u32[]{:S(2)}, u32[]{:S(2)}) collective-permute-start(f32[584,128]{1,0:T(8,128)S(1)} %get-tuple-element.15), channel_id=1, source_target_pairs={{0,64},{1,67},{2,66},{3,65},{4,68},{5,71},{6,70},{7,69},{8,72},{9,... | collective-permute-start | bytes 897032 | tf_op jit(solution)/shard_map/ppermute | solution.py:492
  29.9 17.9 %collective-permute-start.4 = (f32[584,128]{1,0:T(8,128)}, f32[584,128]{1,0:T(8,128)S(1)}, u32[]{:S(2)}, u32[]{:S(2)}) collective-permute-start(f32[584,128]{1,0:T(8,128)} %get-tuple-element.16), channel_id=1, source_target_pairs={{0,80},{1,115},{2,82},{3,113},{4,84},{5,119},{6,86},{7,117},{8,88}... | collective-permute-start | bytes 897032 | tf_op jit(solution)/shard_map/ppermute | solution.py:492
  29.9 17.9 %collective-permute-start.5 = (f32[584,128]{1,0:T(8,128)}, f32[584,128]{1,0:T(8,128)S(1)}, u32[]{:S(2)}, u32[]{:S(2)}) collective-permute-start(f32[584,128]{1,0:T(8,128)} %get-tuple-element.17), channel_id=1, source_target_pairs={{0,4},{1,13},{2,6},{3,15},{4,0},{5,9},{6,2},{7,11},{8,12},{9,5},{1... | collective-permute-start | bytes 897032 | tf_op jit(solution)/shard_map/ppermute | solution.py:492
  31.9 16.0 %collective-permute-start.6 = (f32[584,128]{1,0:T(8,128)S(1)}, f32[584,128]{1,0:T(8,128)S(1)}, u32[]{:S(2)}, u32[]{:S(2)}) collective-permute-start(f32[584,128]{1,0:T(8,128)S(1)} %get-tuple-element.18), channel_id=1, source_target_pairs={{0,20},{1,61},{2,22},{3,63},{4,16},{5,57},{6,18},{7,59},{8,28},{9,... | collective-permute-start | bytes 897032 | tf_op jit(solution)/shard_map/ppermute | solution.py:492
  40.6 9.8 %collective-permute-start.7 = (f32[584,128]{1,0:T(8,128)S(1)}, f32[584,128]{1,0:T(8,128)S(1)}, u32[]{:S(2)}, u32[]{:S(2)}) collective-permute-start(f32[584,128]{1,0:T(8,128)S(1)} %get-tuple-element.19), channel_id=1, source_target_pairs={{0,68},{1,79},{2,70},{3,77},{4,64},{5,75},{6,66},{7,73},{8,76},{9,... | collective-permute-start | bytes 897032 | tf_op jit(solution)/shard_map/ppermute | solution.py:492
  43.0 11.3 %collective-permute-start.8 = (f32[584,128]{1,0:T(8,128)S(1)}, f32[584,128]{1,0:T(8,128)S(1)}, u32[]{:S(2)}, u32[]{:S(2)}) collective-permute-start(f32[584,128]{1,0:T(8,128)S(1)} %get-tuple-element.20), channel_id=1, source_target_pairs={{0,84},{1,127},{2,86},{3,125},{4,80},{5,123},{6,82},{7,121},{8,92}... | collective-permute-start | bytes 897032 | tf_op jit(solution)/shard_map/ppermute | solution.py:492
  44.9 31.3 %copy-start = (s32[128]{0:T(128)S(1)}, s32[128]{0:T(128)}, u32[]{:S(2)}) copy-start(s32[128]{0:T(128)} %damp_ref.1) | copy-start | bytes 1540
  55.3 20.8 %all-to-all-start.1 = ((f32[8,152,128]{2,1,0:T(8,128)}), f32[8,152,128]{2,1,0:T(8,128)S(1)}, u32[]{:S(2)}, u32[]{:S(2)}) async-start(f32[8,152,128]{2,1,0:T(8,128)} %add_odd.1), calls=%async_computation.1 | async-start | bytes 1245184 | tf_op jit(solution)/shard_map/all_to_all | solution.py:495
